TPU v7x, 32 devices: a whole 2x2x4 slice. The times are simulated.
32 devices in a mesh: dp: 4 (over y, x), fsdp: 8 (over z, core).
Axes of the slice: x: 2, y: 2, z: 4, core: 2. Of those that a mesh axis runs over, the one named last changes fastest.
Arguments:
- tokens: bfloat16 [512, 3072], P('dp'), may hold values from -6 to 6
- cotangent: bfloat16 [512, 3072], P('dp'), may hold values from -6 to 6
- routes: int32 [512, 2], P('dp'), may hold values from 0 to 3, all different within a row; in each aligned block of 128 rows (0 to 127, 128 to 255, ...) at most 64 rows name the same one
- router_weight: float32 [512, 2], P('dp'), may hold values from 0.25 to 1
- w_gate: bfloat16 [4, 3072, 8192], P('dp', None, 'fsdp'), may hold values from -0.109375 to 0.109375
- w_up: bfloat16 [4, 3072, 8192], P('dp', None, 'fsdp'), may hold values from -0.109375 to 0.109375
- w_down: bfloat16 [4, 8192, 3072], P('dp', 'fsdp'), may hold values from -0.0625 to 0.0625
Outputs:
- output: bfloat16 [512, 3072], P('dp')
- input_grad: bfloat16 [512, 3072], P('dp')
- grad_gate: bfloat16 [4, 3072, 8192], P('dp', None, 'fsdp')
- grad_up: bfloat16 [4, 3072, 8192], P('dp', None, 'fsdp')
- grad_down: bfloat16 [4, 8192, 3072], P('dp', 'fsdp')
Inputs may be any that keep to these rules, and one draw needn't show every extreme that they name: `routes`: the two experts of a token differ. In the 128 rows of one batch no expert is named by more than 64 rows, a bound that some block reaches in some batches.
All inputs are finite; a program needn't handle non-finite values.
Results may differ from a plain program's by a relative error of at most 0.025.
Values may be sent and summed in bfloat16 or wider, within the bound.
A program may use at most 128 MiB of HBM per device.

v0:
```python
import functools

import jax
import jax.numpy as jnp
from jax import lax
from jax.experimental import pallas as pl
from jax.experimental.pallas import tpu as pltpu
from jax.sharding import PartitionSpec as P

MESH = pl.DeviceIdType.MESH
BF16 = jnp.bfloat16
F32 = jnp.float32
LEAD = (((0,), (0,)), ((), ()))
TRAIL = (((1,), (1,)), ((), ()))


def flip(a, mask):
    bit = 1
    while bit <= mask:
        if mask & bit:
            a = a + bit - 2 * bit * ((a // bit) % 2)
        bit *= 2
    return a


def mm(a, b, dims=(((1,), (0,)), ((), ()))):
    return lax.dot_general(a, b, dims, preferred_element_type=F32)


def routed_kernel(
    n, nz, cap, tile, chunks, lag,
    tokens, cotangent, routes_t, rweight_t, rweight, wg_hbm, wu_hbm, wd_hbm,
    output, input_grad, slots_hbm, hidden_hbm,
    wg, wu, wd, slots, snd, gpre, upre, hid,
    core_snd, core_rcv, own, ret_snd, ret, zacc, zsnd, zrcv, fin,
    w_sem, a_send, a_recv, f_send, f_recv, c_send, c_recv, r_send, r_recv,
    z_send, z_recv, g_send, g_recv, h_send, h_recv, o_sem,
):
    d = lax.axis_index("dp")
    f = lax.axis_index("fsdp")
    c = f % 2
    z = f // 2
    sib = (d, flip(f, 1))
    toks, features = tokens.shape
    half = features // 2
    width = half // chunks
    rows = n * cap
    units = hid.shape[2]
    order = sorted(range(1, n), key=lambda m: -bin(m).count("1"))
    bits = [1 << s for s in range(nz.bit_length() - 1)]

    def remote(src, dst, ssem, rsem, dev):
        return pltpu.make_async_remote_copy(
            src_ref=src, dst_ref=dst, send_sem=ssem, recv_sem=rsem,
            device_id=dev, device_id_type=MESH,
        )

    loads = [
        pltpu.make_async_copy(s, t, w_sem.at[k])
        for k, (s, t) in enumerate(((wg_hbm, wg), (wu_hbm, wu), (wd_hbm, wd)))
    ]
    for load in loads:
        load.start()

    barrier = pltpu.get_barrier_semaphore()
    friends = [(flip(d, m), f) for m in order] + [sib] + [(d, flip(f, 2 * b)) for b in bits]
    for dev in friends:
        pl.semaphore_signal(barrier, inc=1, device_id=dev, device_id_type=MESH)

    slot_row = lax.broadcasted_iota(jnp.int32, (rows, toks), 0)
    e_of = slot_row // cap
    s_of = (slot_row % cap).astype(F32)
    r = routes_t[...]
    hit0 = r[0:1, :] == e_of
    hit1 = r[1:2, :] == e_of
    per_token = jnp.where(hit0 | hit1, 1.0, 0.0).astype(BF16)
    earlier = (
        lax.broadcasted_iota(jnp.int32, (toks, toks), 0)
        < lax.broadcasted_iota(jnp.int32, (toks, toks), 1)
    )
    before = mm(per_token, jnp.where(earlier, 1.0, 0.0).astype(BF16))
    here = before == s_of
    first = jnp.where(hit0 & here, 1.0, 0.0)
    second = jnp.where(hit1 & here, 1.0, 0.0)
    rw = rweight_t[...]
    slot_weight = jnp.sum(first * rw[0:1, :] + second * rw[1:2, :], axis=1, keepdims=True)
    first = first.astype(BF16)
    second = second.astype(BF16)
    picked = first + second

    mine = pl.ds(pl.multiple_of(c * half, 128), half)
    snd[0] = mm(picked, tokens[:, mine]).astype(BF16).reshape(n, cap, half)
    pl.semaphore_wait(barrier, len(friends))

    sends = []

    def dispatch(t):
        for m in order:
            e = flip(d, m)
            cp = remote(snd.at[t, e], slots.at[c, t, d], a_send.at[t, m], a_recv.at[t, m], (e, f))
            cp.start()
            sends.append(cp)
        slots[c, t, d] = snd[t, d]

    def share(t):
        for m in [0] + order:
            b = flip(d, m)
            if m:
                remote(
                    snd.at[t, b], slots.at[c, t, b], a_send.at[t, m], a_recv.at[t, m], (b, f)
                ).wait_recv()
            cp = remote(slots.at[c, t, b], slots.at[c, t, b], f_send.at[t, m], f_recv.at[t, m], sib)
            cp.start()
            sends.append(cp)

    def shared(t):
        for m in [0] + order:
            b = flip(d, m)
            remote(
                slots.at[1 - c, t, b], slots.at[1 - c, t, b], f_send.at[t, m], f_recv.at[t, m], sib
            ).wait_recv()

    dispatch(0)
    snd[1] = (mm(picked, cotangent[:, mine]) * slot_weight).astype(BF16).reshape(n, cap, half)
    dispatch(1)
    share(0)
    shared(0)
    loads[0].wait()
    loads[1].wait()

    def up_step(j, carry):
        cols = pl.ds(pl.multiple_of(j * tile, tile), tile)
        x0 = slots[0, 0].reshape(rows, half)
        x1 = slots[1, 0].reshape(rows, half)
        g = mm(x0, wg[pl.ds(0, half), cols]) + mm(x1, wg[pl.ds(half, half), cols])
        u = mm(x0, wu[pl.ds(0, half), cols]) + mm(x1, wu[pl.ds(half, half), cols])
        gpre[:, cols] = g
        upre[:, cols] = u
        hid[0, :, cols] = (g * jax.nn.sigmoid(g) * u).astype(BF16)
        return carry

    lax.fori_loop(0, units // tile, up_step, 0)
    loads[2].wait()

    def project(t, term):
        def theirs(q, k, carry):
            cols = pl.ds(pl.multiple_of(k * tile, tile), tile)
            at = pl.multiple_of((1 - c) * half + q * width + k * tile, tile)
            v = term(pl.ds(at, tile))
            core_snd[t, q, :, :, cols] = v.astype(BF16).reshape(n, cap, tile)
            return carry

        def ours(q, k, carry):
            cols = pl.ds(pl.multiple_of(k * tile, tile), tile)
            at = pl.multiple_of(c * half + q * width + k * tile, tile)
            own[t, q, :, cols] = term(pl.ds(at, tile))
            return carry

        halves = []
        for q in range(chunks):
            lax.fori_loop(0, width // tile, functools.partial(theirs, q), 0)
            cp = remote(
                core_snd.at[t, q], core_rcv.at[t, q], c_send.at[t, q], c_recv.at[t, q], sib
            )
            cp.start()
            halves.append(cp)
        for q in range(chunks):
            lax.fori_loop(0, width // tile, functools.partial(ours, q), 0)
            halves[q].wait_recv()
            for m in order + [0]:
                b = flip(d, m)
                at = pl.ds(pl.multiple_of(b * cap, 16), cap)
                v = (own[t, q, at, :] + core_rcv[t, q, b].astype(F32)).astype(BF16)
                if m:
                    ret_snd[t, q, b] = v
                    cp = returned(t, q, m, b, d)
                    cp.start()
                    sends.append(cp)
                else:
                    ret[t, q, d] = v
        sends.extend(halves)

    def returned(t, q, m, b, where):
        return remote(
            ret_snd.at[t, q, b],
            ret.at[t, q, where],
            r_send.at[t, q, m],
            r_recv.at[t, q, m],
            (b, f),
        )

    project(0, lambda cols: mm(hid[0], wd[:, cols]))

    share(1)
    shared(1)

    def down_step(j, carry):
        cols = pl.ds(pl.multiple_of(j * tile, tile), tile)
        hdy = mm(slots[0, 1].reshape(rows, half), wd[cols, pl.ds(0, half)], TRAIL) + mm(
            slots[1, 1].reshape(rows, half), wd[cols, pl.ds(half, half)], TRAIL
        )
        g = gpre[:, cols]
        sig = jax.nn.sigmoid(g)
        hid[1, :, cols] = (hdy * upre[:, cols] * sig * (1.0 + g * (1.0 - sig))).astype(BF16)
        hid[2, :, cols] = (hdy * (g * sig)).astype(BF16)
        return carry

    lax.fori_loop(0, units // tile, down_step, 0)
    stores = [
        pltpu.make_async_copy(slots, slots_hbm, o_sem.at[0]),
        pltpu.make_async_copy(hid, hidden_hbm, o_sem.at[1]),
    ]
    for cp in stores:
        cp.start()

    project(1, lambda cols: mm(hid[1], wg[cols, :], TRAIL) + mm(hid[2], wu[cols, :], TRAIL))

    span = toks // nz

    def combine(t, q):
        for m in order:
            b = flip(d, m)
            returned(t, q, m, b, b).wait_recv()
        flat = ret[t, q].reshape(rows, width)
        if t == 0:
            v = rweight[:, 0:1] * mm(first, flat, LEAD) + rweight[:, 1:2] * mm(second, flat, LEAD)
        else:
            v = mm(picked, flat, LEAD)
        zacc[t, q] = v.reshape(nz, span, width)

    def pieces(s, who):
        step = bits[s] * 2
        return [who % step + step * q for q in range(nz // step)]

    base = [sum(nz // (2 * b) for b in bits[:s]) for s in range(len(bits))]

    def summing(t, q, s, k):
        dev = (d, flip(f, 2 * bits[s]))
        return remote(
            zsnd.at[t, q, k], zrcv.at[t, q, k], z_send.at[t, q, k], z_recv.at[t, q, k], dev
        )

    def spreading(t, q, s, k, p):
        dev = (d, flip(f, 2 * bits[s]))
        piece = fin.at[c, t, q, p]
        return remote(piece, piece, g_send.at[t, q, k], g_recv.at[t, q, k], dev)

    def reduce_start(t, q, s):
        for i, p in enumerate(pieces(s, flip(z, bits[s]))):
            k = base[s] + i
            zsnd[t, q, k] = zacc[t, q, p].astype(BF16)
            cp = summing(t, q, s, k)
            cp.start()
            sends.append(cp)

    def reduce_end(t, q, s):
        for i, p in enumerate(pieces(s, z)):
            k = base[s] + i
            summing(t, q, s, k).wait_recv()
            zacc[t, q, p] += zrcv[t, q, k].astype(F32)

    def spread_start(t, q, s):
        for i, p in enumerate(pieces(s, z)):
            cp = spreading(t, q, s, base[s] + i, p)
            cp.start()
            sends.append(cp)

    def spread_end(t, q, s):
        for i, p in enumerate(pieces(s, flip(z, bits[s]))):
            spreading(t, q, s, base[s] + i, p).wait_recv()

    def last(t, q, h):
        piece = fin.at[h, t, q]
        return remote(piece, piece, h_send.at[t, q], h_recv.at[t, q], sib)

    stages = [(reduce_start, reduce_end, s) for s in range(len(bits))]
    stages += [(spread_start, spread_end, s) for s in reversed(range(len(bits)))]

    def advance(t, q, i):
        if i == 0:
            combine(t, q)
        else:
            _, end, s = stages[i - 1]
            end(t, q, s)
        if i == len(bits):
            fin[c, t, q, z] = zacc[t, q, z].astype(BF16)
        if i < len(stages):
            begin, _, s = stages[i]
            begin(t, q, s)
        else:
            cp = last(t, q, c)
            cp.start()
            sends.append(cp)

    todo = [
        (i + lag * t + 0.5 * q, t, q, i) for i in range(len(stages) + 1) for t in range(2) for q in range(chunks)
    ]
    for _, t, q, i in sorted(todo):
        advance(t, q, i)

    for t, result in enumerate((output, input_grad)):
        for q in range(chunks):
            last(t, q, 1 - c).wait_recv()
            for h in range(2):
                at = h * half + q * width
                result[:, at : at + width] = fin[h, t, q].reshape(toks, width)
    for cp in sends:
        cp.wait_send()
    for cp in stores:
        cp.wait()


def grads_kernel(x, dy, hid, grad_gate, grad_up, grad_down):
    rows = hid.shape[1]
    xt = x[0, 0].reshape(rows, x.shape[-1])
    dyt = dy[0, 0].reshape(rows, dy.shape[-1])
    grad_gate[...] = mm(xt, hid[1], LEAD).astype(BF16)
    grad_up[...] = mm(xt, hid[2], LEAD).astype(BF16)
    grad_down[...] = mm(hid[0], dyt, LEAD).astype(BF16)


def fused(tokens, cotangent, routes, router_weight, w_gate, w_up, w_down):
    n = lax.axis_size("dp")
    nz = lax.axis_size("fsdp") // 2
    toks, features = tokens.shape
    cap = capacity_of(toks, n)
    rows = n * cap
    half = features // 2
    units = w_gate.shape[2]
    tile = 256
    chunks = 2
    width = half // chunks
    span = toks // nz
    vmem = pl.BlockSpec(memory_space=pltpu.VMEM)
    hbm = pl.BlockSpec(memory_space=pl.ANY)
    dma = pltpu.SemaphoreType.DMA
    V = pltpu.VMEM
    output, input_grad, slots, hid = pl.pallas_call(
        functools.partial(routed_kernel, n, nz, cap, tile, chunks, 1),
        out_shape=(
            jax.ShapeDtypeStruct((toks, features), BF16),
            jax.ShapeDtypeStruct((toks, features), BF16),
            jax.ShapeDtypeStruct((2, 2, n, cap, half), BF16),
            jax.ShapeDtypeStruct((3, rows, units), BF16),
        ),
        in_specs=[vmem] * 5 + [hbm] * 3,
        out_specs=(vmem, vmem, hbm, hbm),
        scratch_shapes=[
            V((features, units), BF16),
            V((features, units), BF16),
            V((units, features), BF16),
            V((2, 2, n, cap, half), BF16),
            V((2, n, cap, half), BF16),
            V((rows, units), F32),
            V((rows, units), F32),
            V((3, rows, units), BF16),
            V((2, chunks, n, cap, width), BF16),
            V((2, chunks, n, cap, width), BF16),
            V((2, chunks, rows, width), F32),
            V((2, chunks, n, cap, width), BF16),
            V((2, chunks, n, cap, width), BF16),
            V((2, chunks, nz, span, width), F32),
            V((2, chunks, nz, span, width), BF16),
            V((2, chunks, nz, span, width), BF16),
            V((2, 2, chunks, nz, span, width), BF16),
            dma((3,)),
            dma((2, n)), dma((2, n)), dma((2, n)), dma((2, n)),
            dma((2, chunks)), dma((2, chunks)),
            dma((2, chunks, n)), dma((2, chunks, n)),
            dma((2, chunks, nz)), dma((2, chunks, nz)), dma((2, chunks, nz)), dma((2, chunks, nz)),
            dma((2, chunks)), dma((2, chunks)),
            dma((2,)),
        ],
        compiler_params=pltpu.CompilerParams(
            collective_id=0, has_side_effects=True, vmem_limit_bytes=64 * 1000 * 1000
        ),
        name="routed",
    )(tokens, cotangent, routes.T, router_weight.T, router_weight, w_gate[0], w_up[0], w_down[0])

    wide = 512 if half % 512 == 0 else 128
    per = half // wide

    def slot_spec(t):
        return pl.BlockSpec((1, 1, n, cap, wide), lambda i: (i // per, t, 0, 0, i % per))

    grad_gate, grad_up, grad_down = pl.pallas_call(
        grads_kernel,
        grid=(features // wide,),
        out_shape=(
            jax.ShapeDtypeStruct((features, units), BF16),
            jax.ShapeDtypeStruct((features, units), BF16),
            jax.ShapeDtypeStruct((units, features), BF16),
        ),
        in_specs=[
            slot_spec(0),
            slot_spec(1),
            pl.BlockSpec((3, rows, units), lambda i: (0, 0, 0)),
        ],
        out_specs=(
            pl.BlockSpec((wide, units), lambda i: (i, 0)),
            pl.BlockSpec((wide, units), lambda i: (i, 0)),
            pl.BlockSpec((units, wide), lambda i: (0, i)),
        ),
        compiler_params=pltpu.CompilerParams(vmem_limit_bytes=60 * 1000 * 1000),
        name="grads",
    )(slots, slots, hid)
    return output, input_grad, grad_gate[None], grad_up[None], grad_down[None]


def slot_tables(routes, router_weight, experts, capacity):
    expert_ids = jnp.arange(experts, dtype=jnp.int32)
    hit_table = (routes[:, :, None] == expert_ids).astype(jnp.int32)
    per_token = jnp.sum(hit_table, axis=1)
    before = jnp.cumsum(per_token, axis=0) - per_token
    slot_of = jnp.sum(hit_table * before[:, None, :], axis=2)
    slot_ids = jnp.arange(capacity, dtype=jnp.int32)
    placed = hit_table[:, :, :, None] * (slot_of[:, :, None, None] == slot_ids).astype(jnp.int32)
    tok_rows = routes.shape[0]
    flat = placed.reshape(tok_rows, 2, experts * capacity).astype(jnp.float32)
    slot_weight = jnp.sum(flat * router_weight[:, :, None], axis=(0, 1))
    return (flat[:, 0], flat[:, 1], slot_weight)


def on_device(tokens, cotangent, routes, router_weight, w_gate, w_up, w_down):
    experts = lax.axis_size("dp")
    tok_rows, features = tokens.shape
    capacity = max(tok_rows * 3 // 8, tok_rows * 2 // experts, 2)
    local_rows = experts * capacity
    lead = (((0,), (0,)), ((), ()))
    trail = (((1,), (1,)), ((), ()))
    first_pick, second_pick, slot_weight = slot_tables(routes, router_weight, experts, capacity)
    picked = (first_pick + second_pick).astype(jnp.bfloat16)
    send_x = lax.dot_general(picked, tokens, lead, preferred_element_type=jnp.float32).astype(
        jnp.bfloat16
    )
    chosen_dy = lax.dot_general(picked, cotangent, lead, preferred_element_type=jnp.float32)
    send_dy = (chosen_dy * slot_weight[:, None]).astype(jnp.bfloat16)
    arrived_x, arrived_dy = (
        lax.all_to_all(
            send_x.reshape(experts, capacity, features),
            "dp",
            split_axis=0,
            concat_axis=0,
            tiled=True,
        ),
        lax.all_to_all(
            send_dy.reshape(experts, capacity, features),
            "dp",
            split_axis=0,
            concat_axis=0,
            tiled=True,
        ),
    )
    slot_x = arrived_x.reshape(local_rows, features)
    slot_dy = arrived_dy.reshape(local_rows, features)
    gate_w = w_gate[0]
    up_w = w_up[0]
    down_w = w_down[0]
    gate_pre = jnp.dot(slot_x, gate_w, preferred_element_type=jnp.float32)
    up_pre = jnp.dot(slot_x, up_w, preferred_element_type=jnp.float32)
    sigma = jax.nn.sigmoid(gate_pre)
    active = gate_pre * sigma
    hidden = (active * up_pre).astype(jnp.bfloat16)
    out_terms = jnp.dot(hidden, down_w, preferred_element_type=jnp.float32)
    hidden_dy = lax.dot_general(slot_dy, down_w, trail, preferred_element_type=jnp.float32)
    gate_dy = (hidden_dy * up_pre * sigma * (1.0 + gate_pre * (1.0 - sigma))).astype(jnp.bfloat16)
    up_dy = (hidden_dy * active).astype(jnp.bfloat16)
    grad_down = lax.dot_general(hidden, slot_dy, lead, preferred_element_type=jnp.float32).astype(
        jnp.bfloat16
    )
    grad_gate = lax.dot_general(slot_x, gate_dy, lead, preferred_element_type=jnp.float32).astype(
        jnp.bfloat16
    )
    grad_up = lax.dot_general(slot_x, up_dy, lead, preferred_element_type=jnp.float32).astype(
        jnp.bfloat16
    )
    back_terms = lax.dot_general(
        gate_dy, gate_w, trail, preferred_element_type=jnp.float32
    ) + lax.dot_general(up_dy, up_w, trail, preferred_element_type=jnp.float32)
    out_part, back_part = (
        lax.psum_scatter(
            out_terms.reshape(experts, capacity, features).astype(jnp.bfloat16),
            "fsdp",
            scatter_dimension=2,
            tiled=True,
        ).astype(jnp.float32),
        lax.psum_scatter(
            back_terms.reshape(experts, capacity, features).astype(jnp.bfloat16),
            "fsdp",
            scatter_dimension=2,
            tiled=True,
        ).astype(jnp.float32),
    )
    returned_out, returned_dx = (
        lax.all_to_all(
            out_part.astype(jnp.bfloat16), "dp", split_axis=0, concat_axis=0, tiled=True
        ),
        lax.all_to_all(
            back_part.astype(jnp.bfloat16), "dp", split_axis=0, concat_axis=0, tiled=True
        ),
    )
    width = out_part.shape[2]
    flat_out = returned_out.reshape(local_rows, width)
    flat_dx = returned_dx.reshape(local_rows, width)
    first_rows = jnp.dot(
        first_pick.astype(jnp.bfloat16), flat_out, preferred_element_type=jnp.float32
    )
    second_rows = jnp.dot(
        second_pick.astype(jnp.bfloat16), flat_out, preferred_element_type=jnp.float32
    )
    output = (router_weight[:, 0:1] * first_rows + router_weight[:, 1:2] * second_rows).astype(
        jnp.bfloat16
    )
    input_grad = jnp.dot(picked, flat_dx, preferred_element_type=jnp.float32).astype(jnp.bfloat16)
    output, input_grad = (
        lax.all_gather(output, "fsdp", axis=1, tiled=True),
        lax.all_gather(input_grad, "fsdp", axis=1, tiled=True),
    )
    return (output, input_grad, grad_gate[None], grad_up[None], grad_down[None])


def capacity_of(toks, experts):
    return max(toks * 3 // 8, toks * 2 // experts, 2)


def fits(mesh, toks, features, units):
    n, m = mesh.shape["dp"], mesh.shape["fsdp"]
    cap = capacity_of(toks, n)
    powers = n & (n - 1) == 0 and m & (m - 1) == 0 and m >= 4
    whole = features % 1024 == 0 and units % 256 == 0 and cap % 16 == 0 and toks % (8 * m) == 0
    rows = n * cap
    held = 6 * features * units + 2 * rows * (13 * features + 7 * units) + 20 * toks * features
    return powers and whole and held < 56 * 1000 * 1000


def solution(mesh):
    def step(tokens, cotangent, routes, router_weight, w_gate, w_up, w_down):
        body = fused if fits(mesh, *tokens.shape, w_gate.shape[2]) else on_device
        return body(tokens, cotangent, routes, router_weight, w_gate, w_up, w_down)

    return jax.shard_map(
        step,
        mesh=mesh,
        in_specs=(
            P("dp", None),
            P("dp", None),
            P("dp", None),
            P("dp", None),
            P("dp", None, "fsdp"),
            P("dp", None, "fsdp"),
            P("dp", "fsdp", None),
        ),
        out_specs=(
            P("dp", None),
            P("dp", None),
            P("dp", None, "fsdp"),
            P("dp", None, "fsdp"),
            P("dp", "fsdp", None),
        ),
        check_vma=False,
    )
```

profile of v0, /device:TPU:0, one launch (start us, length us, event | category | flops | bytes accessed | tf_op | source)
XLA Modules:
  0.0 83.5 jit_solution(16547921801876587713)
XLA Ops:
  0.6 1.4 %copy.12.rweight = f32[128,2]{1,0:T(8,128)} copy(f32[128,2]{0,1:T(2,128)} %param.10) | data formatting | bytes 2048 | tf_op args[3]
  2.0 69.8 %routed.1 = (bf16[128,3072]{1,0:T(8,128)(2,1)}, bf16[128,3072]{1,0:T(8,128)(2,1)}, bf16[2,2,4,64,1536]{4,3,2,1,0:T(8,128)(2,1)}, bf16[3,256,1024]{2,1,0:T(8,128)(2,1)}) custom-call(bf16[128,3072]{1,0:T(8,128)(2,1)} %tokens.1, bf16[128,3072]{1,0:T(8,128)(2,1)} %cotangent.1, s32[2,128]{1,0:T(2,128)} %bitcast.12, f32[2,128]{1,0:T(2,128)} %bitcast.11, ...), custom_call_target="tpu_custom_call" | custom-call | tf_op jit(solution)/shard_map/routed/pallas_call | solution.py:338
  71.9 0.0 copy-start.1
  71.9 0.0 copy-start
  71.9 9.8 %grads.1 = (bf16[3072,1024]{1,0:T(8,128)(2,1)}, bf16[3072,1024]{1,0:T(8,128)(2,1)}, bf16[1024,3072]{1,0:T(8,128)(2,1)}) custom-call(bf16[2,2,4,64,1536]{4,3,2,1,0:T(8,128)(2,1)} %get-tuple-element.14.x.dy, bf16[2,2,4,64,1536]{4,3,2,1,0:T(8,128)(2,1)} %get-tuple-element.14.x.dy, bf16[3,256,1024]{2,1,0:T(8,128)(2,1)} %get-tuple-element.15.hid), custom_call_target="tpu_custom_call" | custom-call | tf_op jit(solution)/shard_map/grads/pallas_call | solution.py:386
  81.7 0.0 copy-done.1
  81.7 0.9 %copy.15 = bf16[128,3072]{1,0:T(8,128)(2,1)} copy(bf16[128,3072]{1,0:T(8,128)(2,1)S(1)} %copy-done.1) | data formatting | bytes 1572864
  82.6 0.0 copy-done
  82.6 0.9 %copy.16 = bf16[128,3072]{1,0:T(8,128)(2,1)} copy(bf16[128,3072]{1,0:T(8,128)(2,1)S(1)} %copy-done) | data formatting | bytes 1572864
Async XLA Ops:
  71.9 9.8 %copy-start.1 = (bf16[128,3072]{1,0:T(8,128)(2,1)S(1)}, bf16[128,3072]{1,0:T(8,128)(2,1)}, u32[]{:S(2)}) copy-start(bf16[128,3072]{1,0:T(8,128)(2,1)} %get-tuple-element.24) | copy-start | bytes 2359300
  71.9 10.7 %copy-start = (bf16[128,3072]{1,0:T(8,128)(2,1)S(1)}, bf16[128,3072]{1,0:T(8,128)(2,1)}, u32[]{:S(2)}) copy-start(bf16[128,3072]{1,0:T(8,128)(2,1)} %get-tuple-element.25) | copy-start | bytes 2359300
where the time goes:
time: 83.8 us; the launch traced here: 83.5 us
  Pallas kernels  79.6 us (95%)
  local copies, waits for them, and re-layouts  3.18 us (4%)
    pallas_call x1, Pallas kernels, fused(): pl.pallas_call(functools.partial(routed_kernel, n, nz, cap, tile, chunks,...  69.8 us
    pallas_call x1, Pallas kernels, fused(): pl.pallas_call(grads_kernel, grid=(features // wide,), out_shape=(jax.Sha...  9.79 us
    unnamed x7, local copies, waits for them, and re-layouts  3.18 us

commit v1 on v0

v1 whole, which is shorter than its diff:
```python
import functools

import jax
import jax.numpy as jnp
from jax import lax
from jax.experimental import pallas as pl
from jax.experimental.pallas import tpu as pltpu
from jax.sharding import PartitionSpec as P

MESH = pl.DeviceIdType.MESH
BF16 = jnp.bfloat16
F32 = jnp.float32
LEAD = (((0,), (0,)), ((), ()))
TRAIL = (((1,), (1,)), ((), ()))


def flip(a, mask):
    bit = 1
    while bit <= mask:
        if mask & bit:
            a = a + bit - 2 * bit * ((a // bit) % 2)
        bit *= 2
    return a


def xor(v, a, n):
    out = v - v
    bit = 1
    while bit < n:
        x, y = (v // bit) % 2, (a // bit) % 2
        out = out + bit * (x + y - 2 * x * y)
        bit *= 2
    return out


def mm(a, b, dims=(((1,), (0,)), ((), ()))):
    return lax.dot_general(a, b, dims, preferred_element_type=F32)


def routed_kernel(
    n, cap, tile, wide, width,
    tokens_hbm, cotangent_hbm, routes_hbm, rweight_hbm, wg_hbm, wu_hbm, wd_hbm,
    output, input_grad, x_turned, dy_rows, hid_turned, hid_dy,
    tok, cot, rts, rwt, wg, wu, wd, slots, snd, gpre, upre, hid,
    core_snd, core_rcv, own, ret_snd, ret, part, from_outer, joint, from_inner, fin,
    w_sem, a_send, a_recv, d_send, d_recv, f_send, f_recv, c_send, c_recv, r_send, r_recv,
    s_send, s_recv, j_send, j_recv, g_send, g_recv, h_send, h_recv,
):
    d = lax.axis_index("dp")
    f = lax.axis_index("fsdp")
    c = f % 2
    z = f // 2
    sib = (d, flip(f, 1))
    pair = (d, flip(f, 2))
    across = (d, 2 * (3 - z) + c)
    outer = (z % 3) == 0
    inner = (z % 3) != 0
    toks, features = tok.shape
    half = features // 2
    rows = n * cap
    units = gpre.shape[1]
    chunks = half // width
    order = sorted(range(1, n), key=lambda m: -bin(m).count("1"))
    far = order[0]
    near = order[1:]
    share = cap // 2

    def remote(src, dst, ssem, rsem, dev):
        return pltpu.make_async_remote_copy(
            src_ref=src, dst_ref=dst, send_sem=ssem, recv_sem=rsem,
            device_id=dev, device_id_type=MESH,
        )

    barrier = pltpu.get_barrier_semaphore()
    friends = [(flip(d, m), f) for m in order] + [sib, pair, across]
    for dev in friends:
        pl.semaphore_signal(barrier, inc=1, device_id=dev, device_id_type=MESH)

    loads = [
        pltpu.make_async_copy(s, t, w_sem.at[k])
        for k, (s, t) in enumerate(
            (
                (routes_hbm, rts), (rweight_hbm, rwt), (tokens_hbm, tok), (cotangent_hbm, cot),
                (wg_hbm, wg), (wu_hbm, wu), (wd_hbm, wd),
            )
        )
    ]
    for load in loads:
        load.start()
    loads[0].wait()
    loads[1].wait()

    slot_row = lax.broadcasted_iota(jnp.int32, (rows, toks), 0)
    m_of = slot_row // cap
    e_of = xor(m_of, d, n)
    s_of = (slot_row % cap).astype(F32)
    r = rts[...]
    hit0 = r[0:1, :] == e_of
    hit1 = r[1:2, :] == e_of
    per_token = jnp.where(hit0 | hit1, 1.0, 0.0).astype(BF16)
    earlier = (
        lax.broadcasted_iota(jnp.int32, (toks, toks), 0)
        < lax.broadcasted_iota(jnp.int32, (toks, toks), 1)
    )
    before = mm(per_token, jnp.where(earlier, 1.0, 0.0).astype(BF16))
    here = before == s_of
    first = jnp.where(hit0 & here, 1.0, 0.0)
    second = jnp.where(hit1 & here, 1.0, 0.0)
    rw = rwt[...]
    slot_weight = jnp.sum(first * rw[0:1, :] + second * rw[1:2, :], axis=1, keepdims=True)
    picked = (first + second).astype(BF16)
    same = (
        lax.broadcasted_iota(jnp.int32, (toks, toks), 0)
        == lax.broadcasted_iota(jnp.int32, (toks, toks), 1)
    )
    back = mm(jnp.where(same, 1.0, 0.0).astype(BF16), picked, TRAIL).astype(BF16)

    mine = pl.ds(pl.multiple_of(c * half, 128), half)
    other = pl.ds(pl.multiple_of((1 - c) * half, 128), half)

    def build(t):
        src = (tok, cot)[t]
        v = mm(picked, src[:, mine])
        u = mm(picked[:cap], src[:, other])
        if t:
            v = v * slot_weight
            u = u * slot_weight[:cap]
        snd[t] = v.astype(BF16).reshape(n, cap, half)
        slots[c, t, 0] = v[:cap].astype(BF16)
        slots[1 - c, t, 0] = u.astype(BF16)

    held = pl.ds(pl.multiple_of((z % 2) * share, 16), share)
    missing = pl.ds(pl.multiple_of((1 - z % 2) * share, 16), share)
    sends = []

    def start(cp):
        cp.start()
        sends.append((None, cp))

    def direct(t, m):
        dev = (flip(d, m), f)
        if m == far:
            return remote(
                snd.at[t, m, held], slots.at[c, t, m, held], a_send.at[t, m], a_recv.at[t, m], dev
            )
        return remote(snd.at[t, m], slots.at[c, t, m], a_send.at[t, m], a_recv.at[t, m], dev)

    def dispatch(t):
        for m in order:
            start(direct(t, m))

    def relay(t, rows_at):
        piece = slots.at[c, t, far, rows_at]
        return remote(piece, piece, d_send.at[t], d_recv.at[t], pair)

    def forward(t, k, h):
        if k == 0:
            piece = slots.at[h, t, far, held]
        elif k == n:
            piece = slots.at[h, t, far, missing]
        else:
            piece = slots.at[h, t, k]
        return remote(piece, piece, f_send.at[t, k], f_recv.at[t, k], sib)

    def relay_far(t):
        direct(t, far).wait_recv()
        start(relay(t, held))
        start(forward(t, 0, c))

    def collect(t):
        for m in near:
            direct(t, m).wait_recv()
            start(forward(t, m, c))
        relay(t, missing).wait_recv()
        start(forward(t, n, c))

    def collected(t):
        for k in [0] + near + [n]:
            forward(t, k, 1 - c).wait_recv()

    loads[2].wait()
    build(0)
    pl.semaphore_wait(barrier, len(friends))
    dispatch(0)
    loads[3].wait()
    build(1)
    dispatch(1)

    def at_half(h):
        return pl.ds(pl.multiple_of(h * half, 128), half)

    def activate(at, cols, g, u):
        gpre[at, cols] = g
        upre[at, cols] = u
        hid[at, cols] = (g * jax.nn.sigmoid(g) * u).astype(BF16)

    self_rows = pl.ds(0, cap)
    their_rows = pl.ds(cap, rows - cap)

    def self_gate(j, carry):
        cols = pl.ds(pl.multiple_of(j * tile, tile), tile)
        gpre[self_rows, cols] = mm(slots[0, 0, 0], wg[pl.ds(0, half), cols]) + mm(
            slots[1, 0, 0], wg[pl.ds(half, half), cols]
        )
        return carry

    def self_up(j, carry):
        cols = pl.ds(pl.multiple_of(j * tile, tile), tile)
        u = mm(slots[0, 0, 0], wu[pl.ds(0, half), cols]) + mm(
            slots[1, 0, 0], wu[pl.ds(half, half), cols]
        )
        activate(self_rows, cols, gpre[self_rows, cols], u)
        return carry

    def near_half(j, carry):
        cols = pl.ds(pl.multiple_of(j * tile, tile), tile)
        x = slots[c, 0, 1:].reshape(rows - cap, half)
        gpre[their_rows, cols] = mm(x, wg[at_half(c), cols])
        upre[their_rows, cols] = mm(x, wu[at_half(c), cols])
        return carry

    def far_half(j, carry):
        cols = pl.ds(pl.multiple_of(j * tile, tile), tile)
        x = slots[1 - c, 0, 1:].reshape(rows - cap, half)
        g = gpre[their_rows, cols] + mm(x, wg[at_half(1 - c), cols])
        u = upre[their_rows, cols] + mm(x, wu[at_half(1 - c), cols])
        activate(their_rows, cols, g, u)
        return carry

    loads[4].wait()
    with jax.named_scope("self_gate"):
        lax.fori_loop(0, units // tile, self_gate, 0)
    with jax.named_scope("relay0"):
        relay_far(0)
    loads[5].wait()
    with jax.named_scope("self_up"):
        lax.fori_loop(0, units // tile, self_up, 0)
    with jax.named_scope("collect0"):
        collect(0)
    with jax.named_scope("near_half"):
        lax.fori_loop(0, units // tile, near_half, 0)
    with jax.named_scope("collected0"):
        collected(0)
    with jax.named_scope("far_half"):
        lax.fori_loop(0, units // tile, far_half, 0)
    loads[6].wait()
    with jax.named_scope("relay1"):
        relay_far(1)

    def swap(t, q):
        return remote(core_snd.at[t, q], core_rcv.at[t, q], c_send.at[t, q], c_recv.at[t, q], sib)

    def returned(t, q, m):
        return remote(
            ret_snd.at[t, q, m], ret.at[t, q, m], r_send.at[t, q, m], r_recv.at[t, q, m],
            (flip(d, m), f),
        )

    per = wide // width

    def project(t, term, between):
        def theirs(k):
            at = pl.multiple_of((1 - c) * half + k * wide, 128)
            v = term(pl.ds(at, wide)).astype(BF16)
            for i in range(per):
                q = k * per + i
                core_snd[t, q] = v[:, i * width : (i + 1) * width].reshape(n, cap, width)
                start(swap(t, q))

        def ours(k):
            at = pl.multiple_of(c * half + k * wide, 128)
            own[t, k] = term(pl.ds(at, wide))

        def finish(k):
            for i in range(per):
                q = k * per + i
                swap(t, q).wait_recv()
                for m in order + [0]:
                    v = own[t, k, m * cap : (m + 1) * cap, i * width : (i + 1) * width]
                    v = (v + core_rcv[t, q, m].astype(F32)).astype(BF16)
                    if m:
                        ret_snd[t, q, m] = v
                        start(returned(t, q, m))
                    else:
                        ret[t, q, 0] = v

        count = half // wide
        theirs(0)
        ours(0)
        for k in range(1, count):
            theirs(k)
            finish(k - 1)
            ours(k)
        between()
        finish(count - 1)

    with jax.named_scope("project0"):
        project(0, lambda cols: mm(hid[...], wd[:, cols]), lambda: None)
    with jax.named_scope("collect1"):
        collect(1)
        collected(1)

    def down_step(j, carry):
        cols = pl.ds(pl.multiple_of(j * tile, tile), tile)
        hdy = mm(slots[0, 1].reshape(rows, half), wd[cols, pl.ds(0, half)], TRAIL) + mm(
            slots[1, 1].reshape(rows, half), wd[cols, pl.ds(half, half)], TRAIL
        )
        g = gpre[:, cols]
        sig = jax.nn.sigmoid(g)
        hid_dy[0, :, cols] = (hdy * upre[:, cols] * sig * (1.0 + g * (1.0 - sig))).astype(BF16)
        hid_dy[1, :, cols] = (hdy * (g * sig)).astype(BF16)
        return carry

    with jax.named_scope("down"):
        lax.fori_loop(0, units // tile, down_step, 0)
    with jax.named_scope("project1"):
        project(
            1,
            lambda cols: mm(hid_dy[0], wg[cols, :], TRAIL) + mm(hid_dy[1], wu[cols, :], TRAIL),
            lambda: None,
        )

    def outward(t, q):
        return remote(
            part.at[t, q], from_outer.at[t, q], s_send.at[t, q], s_recv.at[t, q], pair
        )

    def middle(t, q):
        return remote(
            joint.at[t, q], from_inner.at[t, q], j_send.at[t, q], j_recv.at[t, q], across
        )

    def spread(t, q):
        piece = fin.at[c, t, q]
        return remote(piece, piece, g_send.at[t, q], g_recv.at[t, q], pair)

    def last(t, q, h):
        piece = fin.at[h, t, q]
        return remote(piece, piece, h_send.at[t, q], h_recv.at[t, q], sib)

    def combine(t, q):
        for m in order:
            returned(t, q, m).wait_recv()
        flat = ret[t, q].reshape(rows, width)
        if t == 0:
            flat = (flat.astype(F32) * slot_weight).astype(BF16)
        part[t, q] = mm(back, flat).astype(BF16)

        @pl.when(outer)
        def _():
            outward(t, q).start()

    def join(t, q):
        @pl.when(inner)
        def _():
            outward(t, q).wait_recv()
            joint[t, q] = (part[t, q].astype(F32) + from_outer[t, q].astype(F32)).astype(BF16)
            middle(t, q).start()

    def settle(t, q):
        @pl.when(inner)
        def _():
            middle(t, q).wait_recv()
            v = joint[t, q].astype(F32) + from_inner[t, q].astype(F32)
            fin[c, t, q] = v.astype(BF16)
            spread(t, q).start()
            last(t, q, c).start()

    def arrive(t, q):
        @pl.when(outer)
        def _():
            spread(t, q).wait_recv()
            last(t, q, c).start()

    def place(t, q):
        last(t, q, 1 - c).wait_recv()
        for h in range(2):
            at = h * half + q * width
            (output, input_grad)[t][:, at : at + width] = fin[h, t, q]

    def turn(k):
        for h in range(2):
            x = slots[h, 0].reshape(rows, half)
            step = half // chunks
            x_turned[h * half + k * step : h * half + (k + 1) * step] = x[
                :, k * step : (k + 1) * step
            ].T
        if k < 2:
            dy_rows[:, k * half : (k + 1) * half] = slots[k, 1].reshape(rows, half)
        if k == chunks - 1:
            hid_turned[...] = hid[...].T

    beat = 8.4 * width / half
    hop = beat + 1.7
    todo = []
    for t in range(2):
        for q in range(chunks):
            at = beat * (t * chunks + q)
            for i, act in enumerate((combine, join, settle, arrive, place)):
                todo.append((at + i * hop, i, t, q, act))
    for _, i, t, q, act in sorted(todo, key=lambda e: e[:4]):
        with jax.named_scope(f"{act.__name__}{t}{q}"):
            act(t, q)
            if i == 0 and t == 0:
                turn(q)

    for _, cp in sends:
        cp.wait_send()
    for t in range(2):
        for q in range(chunks):
            last(t, q, c).wait_send()

            @pl.when(outer)
            def _():
                outward(t, q).wait_send()

            @pl.when(inner)
            def _():
                middle(t, q).wait_send()
                spread(t, q).wait_send()


def grads_kernel(
    step, output, input_grad, x_turned, dy_rows, hid_turned, hid_dy,
    output_hbm, input_grad_hbm, gate_hbm, up_hbm, down_hbm,
    gate, up, down, sem, g_sem,
):
    copies = [
        pltpu.make_async_copy(output, output_hbm, sem.at[0]),
        pltpu.make_async_copy(input_grad, input_grad_hbm, sem.at[1]),
    ]
    for cp in copies:
        cp.start()
    features = x_turned.shape[0]
    units = hid_turned.shape[0]

    def emit(k, at, value, buf, dst):
        buf[pl.ds(at, value.shape[0])] = value.astype(BF16)
        cp = pltpu.make_async_copy(
            buf.at[pl.ds(at, value.shape[0])], dst.at[pl.ds(at, value.shape[0])], g_sem.at[k]
        )
        cp.start()
        copies.append(cp)

    k = 0
    for at in range(0, features, step):
        x = x_turned[at : at + step]
        emit(k, at, mm(x, hid_dy[0]), gate, gate_hbm)
        emit(k + 1, at, mm(x, hid_dy[1]), up, up_hbm)
        k += 2
    rows_at = min(256, units)
    for at in range(0, units, rows_at):
        emit(k, at, mm(hid_turned[at : at + rows_at], dy_rows[...]), down, down_hbm)
        k += 1
    for cp in copies:
        cp.wait()


def fused(tokens, cotangent, routes, router_weight, w_gate, w_up, w_down):
    n = lax.axis_size("dp")
    toks, features = tokens.shape
    cap = capacity_of(toks, n)
    rows = n * cap
    half = features // 2
    units = w_gate.shape[2]
    tile = 512
    wide = 768
    width = 256
    chunks = half // width
    vmem = pl.BlockSpec(memory_space=pltpu.VMEM)
    hbm = pl.BlockSpec(memory_space=pl.ANY)
    dma = pltpu.SemaphoreType.DMA
    V = pltpu.VMEM
    held = pl.pallas_call(
        functools.partial(routed_kernel, n, cap, tile, wide, width),
        out_shape=(
            V((toks, features), BF16),
            V((toks, features), BF16),
            V((features, rows), BF16),
            V((rows, features), BF16),
            V((units, rows), BF16),
            V((2, rows, units), BF16),
        ),
        in_specs=[hbm] * 7,
        out_specs=(vmem,) * 6,
        scratch_shapes=[
            V((toks, features), BF16),
            V((toks, features), BF16),
            V((2, toks), jnp.int32),
            V((2, toks), F32),
            V((features, units), BF16),
            V((features, units), BF16),
            V((units, features), BF16),
            V((2, 2, n, cap, half), BF16),
            V((2, n, cap, half), BF16),
            V((rows, units), F32),
            V((rows, units), F32),
            V((rows, units), BF16),
            V((2, chunks, n, cap, width), BF16),
            V((2, chunks, n, cap, width), BF16),
            V((2, half // wide, rows, wide), F32),
            V((2, chunks, n, cap, width), BF16),
            V((2, chunks, n, cap, width), BF16),
            V((2, chunks, toks, width), BF16),
            V((2, chunks, toks, width), BF16),
            V((2, chunks, toks, width), BF16),
            V((2, chunks, toks, width), BF16),
            V((2, 2, chunks, toks, width), BF16),
            dma((7,)),
            dma((2, n)), dma((2, n)), dma((2,)), dma((2,)),
            dma((2, n + 1)), dma((2, n + 1)),
            dma((2, chunks)), dma((2, chunks)),
            dma((2, chunks, n)), dma((2, chunks, n)),
            dma((2, chunks)), dma((2, chunks)), dma((2, chunks)), dma((2, chunks)),
            dma((2, chunks)), dma((2, chunks)), dma((2, chunks)), dma((2, chunks)),
        ],
        compiler_params=pltpu.CompilerParams(
            collective_id=0, has_side_effects=True, vmem_limit_bytes=54 * 1000 * 1000
        ),
        name="routed",
    )(tokens, cotangent, routes.T, router_weight.T, w_gate[0], w_up[0], w_down[0])

    step = 512
    output, input_grad, grad_gate, grad_up, grad_down = pl.pallas_call(
        functools.partial(grads_kernel, step),
        out_shape=(
            jax.ShapeDtypeStruct((toks, features), BF16),
            jax.ShapeDtypeStruct((toks, features), BF16),
            jax.ShapeDtypeStruct((features, units), BF16),
            jax.ShapeDtypeStruct((features, units), BF16),
            jax.ShapeDtypeStruct((units, features), BF16),
        ),
        in_specs=[vmem] * 6,
        out_specs=(hbm,) * 5,
        scratch_shapes=[
            V((features, units), BF16),
            V((features, units), BF16),
            V((units, features), BF16),
            dma((2,)),
            dma((2 * features // step + units // min(256, units),)),
        ],
        compiler_params=pltpu.CompilerParams(vmem_limit_bytes=50 * 1000 * 1000),
        name="grads",
    )(*held)
    return output, input_grad, grad_gate[None], grad_up[None], grad_down[None]


def slot_tables(routes, router_weight, experts, capacity):
    expert_ids = jnp.arange(experts, dtype=jnp.int32)
    hit_table = (routes[:, :, None] == expert_ids).astype(jnp.int32)
    per_token = jnp.sum(hit_table, axis=1)
    before = jnp.cumsum(per_token, axis=0) - per_token
    slot_of = jnp.sum(hit_table * before[:, None, :], axis=2)
    slot_ids = jnp.arange(capacity, dtype=jnp.int32)
    placed = hit_table[:, :, :, None] * (slot_of[:, :, None, None] == slot_ids).astype(jnp.int32)
    tok_rows = routes.shape[0]
    flat = placed.reshape(tok_rows, 2, experts * capacity).astype(jnp.float32)
    slot_weight = jnp.sum(flat * router_weight[:, :, None], axis=(0, 1))
    return (flat[:, 0], flat[:, 1], slot_weight)


def on_device(tokens, cotangent, routes, router_weight, w_gate, w_up, w_down):
    experts = lax.axis_size("dp")
    tok_rows, features = tokens.shape
    capacity = max(tok_rows * 3 // 8, tok_rows * 2 // experts, 2)
    local_rows = experts * capacity
    lead = (((0,), (0,)), ((), ()))
    trail = (((1,), (1,)), ((), ()))
    first_pick, second_pick, slot_weight = slot_tables(routes, router_weight, experts, capacity)
    picked = (first_pick + second_pick).astype(jnp.bfloat16)
    send_x = lax.dot_general(picked, tokens, lead, preferred_element_type=jnp.float32).astype(
        jnp.bfloat16
    )
    chosen_dy = lax.dot_general(picked, cotangent, lead, preferred_element_type=jnp.float32)
    send_dy = (chosen_dy * slot_weight[:, None]).astype(jnp.bfloat16)
    arrived_x, arrived_dy = (
        lax.all_to_all(
            send_x.reshape(experts, capacity, features),
            "dp",
            split_axis=0,
            concat_axis=0,
            tiled=True,
        ),
        lax.all_to_all(
            send_dy.reshape(experts, capacity, features),
            "dp",
            split_axis=0,
            concat_axis=0,
            tiled=True,
        ),
    )
    slot_x = arrived_x.reshape(local_rows, features)
    slot_dy = arrived_dy.reshape(local_rows, features)
    gate_w = w_gate[0]
    up_w = w_up[0]
    down_w = w_down[0]
    gate_pre = jnp.dot(slot_x, gate_w, preferred_element_type=jnp.float32)
    up_pre = jnp.dot(slot_x, up_w, preferred_element_type=jnp.float32)
    sigma = jax.nn.sigmoid(gate_pre)
    active = gate_pre * sigma
    hidden = (active * up_pre).astype(jnp.bfloat16)
    out_terms = jnp.dot(hidden, down_w, preferred_element_type=jnp.float32)
    hidden_dy = lax.dot_general(slot_dy, down_w, trail, preferred_element_type=jnp.float32)
    gate_dy = (hidden_dy * up_pre * sigma * (1.0 + gate_pre * (1.0 - sigma))).astype(jnp.bfloat16)
    up_dy = (hidden_dy * active).astype(jnp.bfloat16)
    grad_down = lax.dot_general(hidden, slot_dy, lead, preferred_element_type=jnp.float32).astype(
        jnp.bfloat16
    )
    grad_gate = lax.dot_general(slot_x, gate_dy, lead, preferred_element_type=jnp.float32).astype(
        jnp.bfloat16
    )
    grad_up = lax.dot_general(slot_x, up_dy, lead, preferred_element_type=jnp.float32).astype(
        jnp.bfloat16
    )
    back_terms = lax.dot_general(
        gate_dy, gate_w, trail, preferred_element_type=jnp.float32
    ) + lax.dot_general(up_dy, up_w, trail, preferred_element_type=jnp.float32)
    out_part, back_part = (
        lax.psum_scatter(
            out_terms.reshape(experts, capacity, features).astype(jnp.bfloat16),
            "fsdp",
            scatter_dimension=2,
            tiled=True,
        ).astype(jnp.float32),
        lax.psum_scatter(
            back_terms.reshape(experts, capacity, features).astype(jnp.bfloat16),
            "fsdp",
            scatter_dimension=2,
            tiled=True,
        ).astype(jnp.float32),
    )
    returned_out, returned_dx = (
        lax.all_to_all(
            out_part.astype(jnp.bfloat16), "dp", split_axis=0, concat_axis=0, tiled=True
        ),
        lax.all_to_all(
            back_part.astype(jnp.bfloat16), "dp", split_axis=0, concat_axis=0, tiled=True
        ),
    )
    width = out_part.shape[2]
    flat_out = returned_out.reshape(local_rows, width)
    flat_dx = returned_dx.reshape(local_rows, width)
    first_rows = jnp.dot(
        first_pick.astype(jnp.bfloat16), flat_out, preferred_element_type=jnp.float32
    )
    second_rows = jnp.dot(
        second_pick.astype(jnp.bfloat16), flat_out, preferred_element_type=jnp.float32
    )
    output = (router_weight[:, 0:1] * first_rows + router_weight[:, 1:2] * second_rows).astype(
        jnp.bfloat16
    )
    input_grad = jnp.dot(picked, flat_dx, preferred_element_type=jnp.float32).astype(jnp.bfloat16)
    output, input_grad = (
        lax.all_gather(output, "fsdp", axis=1, tiled=True),
        lax.all_gather(input_grad, "fsdp", axis=1, tiled=True),
    )
    return (output, input_grad, grad_gate[None], grad_up[None], grad_down[None])


def capacity_of(toks, experts):
    return max(toks * 3 // 8, toks * 2 // experts, 2)


def fits(mesh, toks, features, units):
    n, m = mesh.shape["dp"], mesh.shape["fsdp"]
    cap = capacity_of(toks, n)
    lines = n == 4 and m == 8
    whole = features % 1536 == 0 and units % 512 == 0 and cap % 32 == 0 and toks % 128 == 0
    rows = n * cap
    held = 6 * features * units + 2 * rows * (15 * features + 8 * units) + 20 * toks * features
    return lines and whole and held < 56 * 1000 * 1000


def solution(mesh):
    def step(tokens, cotangent, routes, router_weight, w_gate, w_up, w_down):
        body = fused if fits(mesh, *tokens.shape, w_gate.shape[2]) else on_device
        return body(tokens, cotangent, routes, router_weight, w_gate, w_up, w_down)

    return jax.shard_map(
        step,
        mesh=mesh,
        in_specs=(
            P("dp", None),
            P("dp", None),
            P("dp", None),
            P("dp", None),
            P("dp", None, "fsdp"),
            P("dp", None, "fsdp"),
            P("dp", "fsdp", None),
        ),
        out_specs=(
            P("dp", None),
            P("dp", None),
            P("dp", None, "fsdp"),
            P("dp", None, "fsdp"),
            P("dp", "fsdp", None),
        ),
        check_vma=False,
    )
```

time: 83.8 us -> 68.9 us (0.82)
  Pallas kernels: 79.6 us -> 67.9 us
  local copies, waits for them, and re-layouts: 3.18 us -> 0 us
    pallas_call x2, Pallas kernels: 79.6 us -> 67.9 us  [the longest x1 60.3 us: fused(): pl.pallas_call(functools.partial(routed_kernel, n, cap, tile, wide, width...]
    unnamed x7 -> x0, local copies, waits for them, and re-layouts: 3.18 us -> none
where the time goes in v1:
time: 68.9 us; the launch traced here: 68.7 us
  Pallas kernels  67.9 us (99%)
  between operations  0.8 us (1%)
    pallas_call x1, Pallas kernels, fused(): pl.pallas_call(functools.partial(routed_kernel, n, cap, tile, wide, width...  60.3 us
    pallas_call x1, Pallas kernels, fused(): pl.pallas_call(functools.partial(grads_kernel, step), out_shape=(jax.Shap...  7.54 us

profile of v1, /device:TPU:0, one launch (start us, length us, event | category | flops | bytes accessed | tf_op | source)
XLA Modules:
  0.0 68.7 jit_solution(8323574892375743392)
XLA Ops:
  0.6 60.3 %routed.1 = (bf16[128,3072]{1,0:T(8,128)(2,1)S(1)}, bf16[128,3072]{1,0:T(8,128)(2,1)S(1)}, bf16[3072,256]{1,0:T(8,128)(2,1)S(1)}, bf16[256,3072]{1,0:T(8,128)(2,...) custom-call(bf16[128,3072]{1,0:T(8,128)(2,1)} %tokens_hbm.1, bf16[128,3072]{1,0:T(8,128)(2,1)} %cotangent_hbm.1, ...), custom_call_target="tpu_custom_call" | custom-call | tf_op jit(solution)/shard_map/routed/pallas_call | solution.py:474
  61.0 7.5 %grads.1 = (bf16[128,3072]{1,0:T(8,128)(2,1)}, bf16[128,3072]{1,0:T(8,128)(2,1)}, bf16[3072,1024]{1,0:T(8,128)(2,1)}, bf16[3072,1024]{1,0:T(8,128)(2,1)}, bf16[1024,3072]{1,0:T(8,128)(2,1)}) custom-call(bf16[128,3072]{1,0:T(8,128)(2,1)S(1)} %get-tuple-element.16.output, bf16[128,3072]{1,0:T(8,128)(2,1)S(1)} %get-tuple-element.17.input_grad, ...), custom_call_target="tpu_custom_call" | custom-call | tf_op jit(solution)/shard_map/grads/pallas_call | solution.py:524

commit v2 on v1

--- a/solution.py
+++ b/solution.py
@@ -38,13 +38,13 @@
 
 
 def routed_kernel(
-    n, cap, tile, wide, width,
+    n, cap, tile, wide, pieces,
     tokens_hbm, cotangent_hbm, routes_hbm, rweight_hbm, wg_hbm, wu_hbm, wd_hbm,
     output, input_grad, x_turned, dy_rows, hid_turned, hid_dy,
-    tok, cot, rts, rwt, wg, wu, wd, slots, snd, gpre, upre, hid,
+    tok, cot, rts, rwt, wg, wu, wd, slots, snd, gpre, upre, hacc, hid,
     core_snd, core_rcv, own, ret_snd, ret, part, from_outer, joint, from_inner, fin,
     w_sem, a_send, a_recv, d_send, d_recv, f_send, f_recv, c_send, c_recv, r_send, r_recv,
-    s_send, s_recv, j_send, j_recv, g_send, g_recv, h_send, h_recv,
+    s_send, s_recv, j_send, j_recv, h_send, h_recv,
 ):
     d = lax.axis_index("dp")
     f = lax.axis_index("fsdp")
@@ -59,7 +59,7 @@
     half = features // 2
     rows = n * cap
     units = gpre.shape[1]
-    chunks = half // width
+    slabs = half // 128
     order = sorted(range(1, n), key=lambda m: -bin(m).count("1"))
     far = order[0]
     near = order[1:]
@@ -87,8 +87,9 @@
     ]
     for load in loads:
         load.start()
-    loads[0].wait()
-    loads[1].wait()
+    with jax.named_scope('w_small'):
+        loads[0].wait()
+        loads[1].wait()
 
     slot_row = lax.broadcasted_iota(jnp.int32, (rows, toks), 0)
     m_of = slot_row // cap
@@ -131,59 +132,69 @@
 
     held = pl.ds(pl.multiple_of((z % 2) * share, 16), share)
     missing = pl.ds(pl.multiple_of((1 - z % 2) * share, 16), share)
-    sends = []
-
-    def start(cp):
-        cp.start()
-        sends.append((None, cp))
-
-    def direct(t, m):
+    parts = 2
+    depth = half // parts
+
+    def part_of(j):
+        return pl.ds(j * depth, depth)
+
+    def direct(t, m, j):
         dev = (flip(d, m), f)
         if m == far:
             return remote(
-                snd.at[t, m, held], slots.at[c, t, m, held], a_send.at[t, m], a_recv.at[t, m], dev
+                snd.at[t, m, held, part_of(j)], slots.at[c, t, m, held, part_of(j)],
+                a_send.at[t, 0], a_recv.at[t, j, 0], dev,
             )
-        return remote(snd.at[t, m], slots.at[c, t, m], a_send.at[t, m], a_recv.at[t, m], dev)
+        return remote(
+            snd.at[t, m, :, part_of(j)], slots.at[c, t, m, :, part_of(j)],
+            a_send.at[t, 1], a_recv.at[t, j, m], dev,
+        )
 
     def dispatch(t):
-        for m in order:
-            start(direct(t, m))
-
-    def relay(t, rows_at):
-        piece = slots.at[c, t, far, rows_at]
-        return remote(piece, piece, d_send.at[t], d_recv.at[t], pair)
-
-    def forward(t, k, h):
+        for j in range(parts):
+            direct(t, far, j).start()
+        for j in range(parts):
+            for m in near:
+                direct(t, m, j).start()
+
+    def relay(t, j, rows_at):
+        piece = slots.at[c, t, far, rows_at, part_of(j)]
+        return remote(piece, piece, d_send.at[t], d_recv.at[t, j], pair)
+
+    def forward(t, j, k):
         if k == 0:
-            piece = slots.at[h, t, far, held]
+            piece = slots.at[c, t, far, held, part_of(j)]
         elif k == n:
-            piece = slots.at[h, t, far, missing]
+            piece = slots.at[c, t, far, missing, part_of(j)]
         else:
-            piece = slots.at[h, t, k]
-        return remote(piece, piece, f_send.at[t, k], f_recv.at[t, k], sib)
-
-    def relay_far(t):
-        direct(t, far).wait_recv()
-        start(relay(t, held))
-        start(forward(t, 0, c))
-
-    def collect(t):
+            piece = slots.at[c, t, k, :, part_of(j)]
+        return remote(piece, piece, f_send.at[t], f_recv.at[t, j], sib)
+
+    def relay_far(t, j):
+        direct(t, far, j).wait_recv()
+        relay(t, j, held).start()
+        forward(t, j, 0).start()
+
+    def collect(t, j):
         for m in near:
-            direct(t, m).wait_recv()
-            start(forward(t, m, c))
-        relay(t, missing).wait_recv()
-        start(forward(t, n, c))
-
-    def collected(t):
-        for k in [0] + near + [n]:
-            forward(t, k, 1 - c).wait_recv()
+            direct(t, m, j).wait_recv()
+            forward(t, j, m).start()
+        relay(t, j, missing).wait_recv()
+        forward(t, j, n).start()
+
+    def collected(t, j):
+        theirs = slots.at[1 - c, t, pl.ds(1, n - 1), :, part_of(j)]
+        remote(theirs, theirs, f_send.at[t], f_recv.at[t, j], sib).wait_recv()
 
     loads[2].wait()
-    build(0)
-    pl.semaphore_wait(barrier, len(friends))
+    with jax.named_scope("build0"):
+        build(0)
+    with jax.named_scope("w_barrier"):
+        pl.semaphore_wait(barrier, len(friends))
     dispatch(0)
     loads[3].wait()
-    build(1)
+    with jax.named_scope("build1"):
+        build(1)
     dispatch(1)
 
     def at_half(h):
@@ -198,171 +209,189 @@
     their_rows = pl.ds(cap, rows - cap)
 
     def self_gate(j, carry):
-        cols = pl.ds(pl.multiple_of(j * tile, tile), tile)
+        cols = pl.ds(j * tile, tile)
         gpre[self_rows, cols] = mm(slots[0, 0, 0], wg[pl.ds(0, half), cols]) + mm(
             slots[1, 0, 0], wg[pl.ds(half, half), cols]
         )
         return carry
 
     def self_up(j, carry):
-        cols = pl.ds(pl.multiple_of(j * tile, tile), tile)
+        cols = pl.ds(j * tile, tile)
         u = mm(slots[0, 0, 0], wu[pl.ds(0, half), cols]) + mm(
             slots[1, 0, 0], wu[pl.ds(half, half), cols]
         )
         activate(self_rows, cols, gpre[self_rows, cols], u)
         return carry
 
-    def near_half(j, carry):
-        cols = pl.ds(pl.multiple_of(j * tile, tile), tile)
-        x = slots[c, 0, 1:].reshape(rows - cap, half)
-        gpre[their_rows, cols] = mm(x, wg[at_half(c), cols])
-        upre[their_rows, cols] = mm(x, wu[at_half(c), cols])
+    def near_part(h, k, j, carry):
+        cols = pl.ds(j * tile, tile)
+        x = slots[h, 0, 1:, :, part_of(k)].reshape(rows - cap, depth)
+        at = pl.ds(pl.multiple_of(h * half + k * depth, 128), depth)
+        gpre[their_rows, cols] += mm(x, wg[at, cols])
+        upre[their_rows, cols] += mm(x, wu[at, cols])
         return carry
 
-    def far_half(j, carry):
-        cols = pl.ds(pl.multiple_of(j * tile, tile), tile)
-        x = slots[1 - c, 0, 1:].reshape(rows - cap, half)
-        g = gpre[their_rows, cols] + mm(x, wg[at_half(1 - c), cols])
-        u = upre[their_rows, cols] + mm(x, wu[at_half(1 - c), cols])
+    def first_part(j, carry):
+        cols = pl.ds(j * tile, tile)
+        x = slots[c, 0, 1:, :, part_of(0)].reshape(rows - cap, depth)
+        at = pl.ds(pl.multiple_of(c * half, 128), depth)
+        gpre[their_rows, cols] = mm(x, wg[at, cols])
+        upre[their_rows, cols] = mm(x, wu[at, cols])
+        return carry
+
+    def last_part(j, carry):
+        cols = pl.ds(j * tile, tile)
+        x = slots[1 - c, 0, 1:, :, part_of(parts - 1)].reshape(rows - cap, depth)
+        at = pl.ds(pl.multiple_of((1 - c) * half + (parts - 1) * depth, 128), depth)
+        g = gpre[their_rows, cols] + mm(x, wg[at, cols])
+        u = upre[their_rows, cols] + mm(x, wu[at, cols])
         activate(their_rows, cols, g, u)
         return carry
 
+    def each_tile(body):
+        for j in range(units // tile):
+            body(j, 0)
+
     loads[4].wait()
     with jax.named_scope("self_gate"):
-        lax.fori_loop(0, units // tile, self_gate, 0)
-    with jax.named_scope("relay0"):
-        relay_far(0)
+        each_tile(self_gate)
     loads[5].wait()
     with jax.named_scope("self_up"):
-        lax.fori_loop(0, units // tile, self_up, 0)
-    with jax.named_scope("collect0"):
-        collect(0)
-    with jax.named_scope("near_half"):
-        lax.fori_loop(0, units // tile, near_half, 0)
-    with jax.named_scope("collected0"):
-        collected(0)
-    with jax.named_scope("far_half"):
-        lax.fori_loop(0, units // tile, far_half, 0)
+        each_tile(self_up)
+    with jax.named_scope("relay0"):
+        relay_far(0, 0)
+        relay_far(0, 1)
+    with jax.named_scope("collect00"):
+        collect(0, 0)
+    with jax.named_scope("own0"):
+        each_tile(first_part)
+    with jax.named_scope("collect01"):
+        collect(0, 1)
+    with jax.named_scope("own1"):
+        each_tile(functools.partial(near_part, c, 1))
+    with jax.named_scope("collected00"):
+        collected(0, 0)
+    with jax.named_scope("relay10"):
+        relay_far(1, 0)
+    with jax.named_scope("sib0"):
+        each_tile(functools.partial(near_part, 1 - c, 0))
+    with jax.named_scope("collected01"):
+        collected(0, 1)
+    with jax.named_scope("relay11"):
+        relay_far(1, 1)
+    with jax.named_scope("sib1"):
+        each_tile(last_part)
     loads[6].wait()
-    with jax.named_scope("relay1"):
-        relay_far(1)
-
-    def swap(t, q):
-        return remote(core_snd.at[t, q], core_rcv.at[t, q], c_send.at[t, q], c_recv.at[t, q], sib)
+
+    def swap(t, k):
+        return remote(core_snd.at[t, k], core_rcv.at[t, k], c_send.at[t], c_recv.at[t, k], sib)
 
     def returned(t, q, m):
+        at = pl.ds(*pieces[t][q])
         return remote(
-            ret_snd.at[t, q, m], ret.at[t, q, m], r_send.at[t, q, m], r_recv.at[t, q, m],
-            (flip(d, m), f),
+            ret_snd.at[t, at, m], ret.at[t, at, m], r_send.at[t], r_recv.at[t, q], (flip(d, m), f)
         )
 
-    per = wide // width
-
-    def project(t, term, between):
-        def theirs(k):
-            at = pl.multiple_of((1 - c) * half + k * wide, 128)
-            v = term(pl.ds(at, wide)).astype(BF16)
-            for i in range(per):
-                q = k * per + i
-                core_snd[t, q] = v[:, i * width : (i + 1) * width].reshape(n, cap, width)
-                start(swap(t, q))
-
-        def ours(k):
-            at = pl.multiple_of(c * half + k * wide, 128)
-            own[t, k] = term(pl.ds(at, wide))
-
-        def finish(k):
-            for i in range(per):
-                q = k * per + i
-                swap(t, q).wait_recv()
-                for m in order + [0]:
-                    v = own[t, k, m * cap : (m + 1) * cap, i * width : (i + 1) * width]
-                    v = (v + core_rcv[t, q, m].astype(F32)).astype(BF16)
-                    if m:
-                        ret_snd[t, q, m] = v
-                        start(returned(t, q, m))
-                    else:
-                        ret[t, q, 0] = v
-
-        count = half // wide
-        theirs(0)
-        ours(0)
-        for k in range(1, count):
-            theirs(k)
-            finish(k - 1)
-            ours(k)
-        between()
-        finish(count - 1)
-
-    with jax.named_scope("project0"):
-        project(0, lambda cols: mm(hid[...], wd[:, cols]), lambda: None)
-    with jax.named_scope("collect1"):
-        collect(1)
-        collected(1)
-
-    def down_step(j, carry):
-        cols = pl.ds(pl.multiple_of(j * tile, tile), tile)
-        hdy = mm(slots[0, 1].reshape(rows, half), wd[cols, pl.ds(0, half)], TRAIL) + mm(
-            slots[1, 1].reshape(rows, half), wd[cols, pl.ds(half, half)], TRAIL
-        )
-        g = gpre[:, cols]
-        sig = jax.nn.sigmoid(g)
-        hid_dy[0, :, cols] = (hdy * upre[:, cols] * sig * (1.0 + g * (1.0 - sig))).astype(BF16)
-        hid_dy[1, :, cols] = (hdy * (g * sig)).astype(BF16)
-        return carry
-
-    with jax.named_scope("down"):
-        lax.fori_loop(0, units // tile, down_step, 0)
-    with jax.named_scope("project1"):
-        project(
-            1,
-            lambda cols: mm(hid_dy[0], wg[cols, :], TRAIL) + mm(hid_dy[1], wu[cols, :], TRAIL),
-            lambda: None,
-        )
+    per = wide // 128
+
+    def term(t, cols):
+        if t == 0:
+            return mm(hid[...], wd[:, cols])
+        return mm(hid_dy[0], wg[cols, :], TRAIL) + mm(hid_dy[1], wu[cols, :], TRAIL)
+
+    def theirs(t, k):
+        at = pl.multiple_of((1 - c) * half + k * wide, 128)
+        core_snd[t, k] = term(t, pl.ds(at, wide)).astype(BF16)
+        swap(t, k).start()
+
+    def ours(t, k):
+        at = pl.multiple_of(c * half + k * wide, 128)
+        own[t, k] = term(t, pl.ds(at, wide))
+
+    def finish(t, k):
+        swap(t, k).wait_recv()
+        for q, (g0, count) in enumerate(pieces[t]):
+            if g0 // per != k:
+                continue
+            for m in order + [0]:
+                for g in range(g0, g0 + count):
+                    at = (g - k * per) * 128
+                    rows_at = pl.ds(m * cap, cap)
+                    v = own[t, k, rows_at, at : at + 128] + core_rcv[
+                        t, k, rows_at, at : at + 128
+                    ].astype(F32)
+                    (ret_snd if m else ret)[t, g, m] = v.astype(BF16)
+                if m:
+                    returned(t, q, m).start()
+
+    def down_own():
+        def body(j, carry):
+            cols = pl.ds(j * tile, tile)
+            hacc[:, cols] = mm(slots[c, 1].reshape(rows, half), wd[cols, mine], TRAIL)
+            return carry
+
+        each_tile(body)
+
+    def down_rest():
+        def body(j, carry):
+            cols = pl.ds(j * tile, tile)
+            hdy = hacc[:, cols] + mm(slots[1 - c, 1].reshape(rows, half), wd[cols, other], TRAIL)
+            g = gpre[:, cols]
+            sig = jax.nn.sigmoid(g)
+            hid_dy[0, :, cols] = (hdy * upre[:, cols] * sig * (1.0 + g * (1.0 - sig))).astype(BF16)
+            hid_dy[1, :, cols] = (hdy * (g * sig)).astype(BF16)
+            return carry
+
+        each_tile(body)
 
     def outward(t, q):
-        return remote(
-            part.at[t, q], from_outer.at[t, q], s_send.at[t, q], s_recv.at[t, q], pair
-        )
+        at = pl.ds(*pieces[t][q])
+        return remote(part.at[t, at], from_outer.at[t, at], s_send.at[t], s_recv.at[t, q], pair)
 
     def middle(t, q):
-        return remote(
-            joint.at[t, q], from_inner.at[t, q], j_send.at[t, q], j_recv.at[t, q], across
-        )
+        at = pl.ds(*pieces[t][q])
+        return remote(joint.at[t, at], from_inner.at[t, at], j_send.at[t], j_recv.at[t, q], across)
 
     def spread(t, q):
-        piece = fin.at[c, t, q]
-        return remote(piece, piece, g_send.at[t, q], g_recv.at[t, q], pair)
+        piece = fin.at[c, t, pl.ds(*pieces[t][q])]
+        return remote(piece, piece, s_send.at[t], s_recv.at[t, q], pair)
 
     def last(t, q, h):
-        piece = fin.at[h, t, q]
-        return remote(piece, piece, h_send.at[t, q], h_recv.at[t, q], sib)
+        piece = fin.at[h, t, pl.ds(*pieces[t][q])]
+        return remote(piece, piece, h_send.at[t], h_recv.at[t, q], sib)
 
     def combine(t, q):
-        for m in order:
-            returned(t, q, m).wait_recv()
-        flat = ret[t, q].reshape(rows, width)
+        g0, count = pieces[t][q]
+        landed = ret.at[t, pl.ds(g0, count), pl.ds(1, n - 1)]
+        remote(landed, landed, r_send.at[t], r_recv.at[t, q], sib).wait_recv()
+        flat = jnp.concatenate([ret[t, g].reshape(rows, 128) for g in range(g0, g0 + count)], axis=1)
         if t == 0:
             flat = (flat.astype(F32) * slot_weight).astype(BF16)
-        part[t, q] = mm(back, flat).astype(BF16)
+        v = mm(back, flat).astype(BF16)
+        for i in range(count):
+            part[t, g0 + i] = v[:, i * 128 : (i + 1) * 128]
 
         @pl.when(outer)
         def _():
             outward(t, q).start()
 
     def join(t, q):
+        at = pl.ds(*pieces[t][q])
+
         @pl.when(inner)
         def _():
             outward(t, q).wait_recv()
-            joint[t, q] = (part[t, q].astype(F32) + from_outer[t, q].astype(F32)).astype(BF16)
+            joint[t, at] = (part[t, at].astype(F32) + from_outer[t, at].astype(F32)).astype(BF16)
             middle(t, q).start()
 
     def settle(t, q):
+        at = pl.ds(*pieces[t][q])
+
         @pl.when(inner)
         def _():
             middle(t, q).wait_recv()
-            v = joint[t, q].astype(F32) + from_inner[t, q].astype(F32)
-            fin[c, t, q] = v.astype(BF16)
+            v = joint[t, at].astype(F32) + from_inner[t, at].astype(F32)
+            fin[c, t, at] = v.astype(BF16)
             spread(t, q).start()
             last(t, q, c).start()
 
@@ -374,50 +403,95 @@
 
     def place(t, q):
         last(t, q, 1 - c).wait_recv()
+        g0, count = pieces[t][q]
         for h in range(2):
-            at = h * half + q * width
-            (output, input_grad)[t][:, at : at + width] = fin[h, t, q]
+            for g in range(g0, g0 + count):
+                at = h * half + g * 128
+                (output, input_grad)[t][:, at : at + 128] = fin[h, t, g]
 
     def turn(k):
-        for h in range(2):
-            x = slots[h, 0].reshape(rows, half)
-            step = half // chunks
-            x_turned[h * half + k * step : h * half + (k + 1) * step] = x[
-                :, k * step : (k + 1) * step
-            ].T
-        if k < 2:
-            dy_rows[:, k * half : (k + 1) * half] = slots[k, 1].reshape(rows, half)
-        if k == chunks - 1:
+        h, i = k // 3, k % 3
+        step = half // 3
+        x = slots[h, 0].reshape(rows, half)[:, i * step : (i + 1) * step]
+        x_turned[h * half + i * step : h * half + (i + 1) * step] = x.T
+        if i == 0:
+            dy_rows[:, h * half : (h + 1) * half] = slots[h, 1].reshape(rows, half)
+        if k == 5:
             hid_turned[...] = hid[...].T
 
-    beat = 8.4 * width / half
-    hop = beat + 1.7
-    todo = []
+    def gather():
+        for j in range(parts):
+            collect(1, j)
+
+    def gathered():
+        for j in range(parts):
+            collected(1, j)
+
+    count = half // wide
+    plan = []
+
+    def at(when, what, *args):
+        plan.append((when, len(plan), what, args))
+
+    def project(t, when, unit, end):
+        for k in range(count):
+            at(when + 2 * k * unit, theirs, t, k)
+            if k:
+                at(when + 2 * k * unit + 0.01, finish, t, k - 1)
+            at(when + (2 * k + 1) * unit, ours, t, k)
+        at(end, finish, t, count - 1)
+
+    beat = 0.7
+    lag = 2.3
+    project(0, 0.0, 0.46, 4.2)
+    at(2.9, gather)
+    at(3.0, down_own)
+    at(4.25, gathered)
+    at(4.3, down_rest)
+    project(1, 5.6, 0.76, 11.2)
+    for k in range(6):
+        at(12.0 + k, turn, k)
+    free = [0.0] * 4
+    ready = [1.5, 8.2]
     for t in range(2):
-        for q in range(chunks):
-            at = beat * (t * chunks + q)
-            for i, act in enumerate((combine, join, settle, arrive, place)):
-                todo.append((at + i * hop, i, t, q, act))
-    for _, i, t, q, act in sorted(todo, key=lambda e: e[:4]):
-        with jax.named_scope(f"{act.__name__}{t}{q}"):
-            act(t, q)
-            if i == 0 and t == 0:
-                turn(q)
-
-    for _, cp in sends:
-        cp.wait_send()
-    for t in range(2):
-        for q in range(chunks):
-            last(t, q, c).wait_send()
+        for q, (g0, size) in enumerate(pieces[t]):
+            when = ready[t]
+            for i, act in enumerate((combine, join, settle, arrive)):
+                free[i] = max(free[i], when) + beat * size
+                when = free[i] + lag + (1.0 if i == 0 else 0.0)
+                at(when + (1.5 if act is arrive else 0.0), act, t, q)
+            at(when + 2.8, place, t, q)
+    for _, _, what, args in sorted(plan, key=lambda e: e[:2]):
+        with jax.named_scope(what.__name__ + "".join(str(a) for a in args)):
+            what(*args)
+
+    with jax.named_scope("drain"):
+        for t in range(2):
+            sent = snd.at[t, far, held]
+            remote(sent, sent, a_send.at[t, 0], a_recv.at[t, 0, 0], sib).wait_send()
+            sent = snd.at[t, pl.ds(near[0], len(near))]
+            remote(sent, sent, a_send.at[t, 1], a_recv.at[t, 0, 1], sib).wait_send()
+            sent = slots.at[c, t, far, held]
+            remote(sent, sent, d_send.at[t], d_recv.at[t, 0], pair).wait_send()
+            sent = slots.at[c, t, pl.ds(1, n - 1)]
+            remote(sent, sent, f_send.at[t], f_recv.at[t, 0], sib).wait_send()
+            remote(core_snd.at[t], core_rcv.at[t], c_send.at[t], c_recv.at[t, 0], sib).wait_send()
+            sent = ret_snd.at[t, :, pl.ds(1, n - 1)]
+            remote(sent, sent, r_send.at[t], r_recv.at[t, 0], sib).wait_send()
+            sent = fin.at[c, t]
+            remote(sent, sent, h_send.at[t], h_recv.at[t, 0], sib).wait_send()
 
             @pl.when(outer)
             def _():
-                outward(t, q).wait_send()
+                sent = part.at[t]
+                remote(sent, sent, s_send.at[t], s_recv.at[t, 0], pair).wait_send()
 
             @pl.when(inner)
             def _():
-                middle(t, q).wait_send()
-                spread(t, q).wait_send()
+                sent = joint.at[t]
+                remote(sent, sent, j_send.at[t], j_recv.at[t, 0], across).wait_send()
+                sent = fin.at[c, t]
+                remote(sent, sent, s_send.at[t], s_recv.at[t, 0], pair).wait_send()
 
 
 def grads_kernel(
@@ -464,15 +538,17 @@
     half = features // 2
     units = w_gate.shape[2]
     tile = 512
-    wide = 768
-    width = 256
-    chunks = half // width
+    wide = 512
+    slabs = half // 128
+    even = [(g, 2) for g in range(0, slabs, 2)]
+    pieces = ([(0, 1), (1, 1)] + even[1:], even[:-1] + [(slabs - 2, 1), (slabs - 1, 1)])
+    most = max(len(p) for p in pieces)
     vmem = pl.BlockSpec(memory_space=pltpu.VMEM)
     hbm = pl.BlockSpec(memory_space=pl.ANY)
     dma = pltpu.SemaphoreType.DMA
     V = pltpu.VMEM
     held = pl.pallas_call(
-        functools.partial(routed_kernel, n, cap, tile, wide, width),
+        functools.partial(routed_kernel, n, cap, tile, wide, pieces),
         out_shape=(
             V((toks, features), BF16),
             V((toks, features), BF16),
@@ -495,24 +571,24 @@
             V((2, n, cap, half), BF16),
             V((rows, units), F32),
             V((rows, units), F32),
+            V((rows, units), F32),
             V((rows, units), BF16),
-            V((2, chunks, n, cap, width), BF16),
-            V((2, chunks, n, cap, width), BF16),
+            V((2, half // wide, rows, wide), BF16),
+            V((2, half // wide, rows, wide), BF16),
             V((2, half // wide, rows, wide), F32),
-            V((2, chunks, n, cap, width), BF16),
-            V((2, chunks, n, cap, width), BF16),
-            V((2, chunks, toks, width), BF16),
-            V((2, chunks, toks, width), BF16),
-            V((2, chunks, toks, width), BF16),
-            V((2, chunks, toks, width), BF16),
-            V((2, 2, chunks, toks, width), BF16),
+            V((2, slabs, n, cap, 128), BF16),
+            V((2, slabs, n, cap, 128), BF16),
+            V((2, slabs, toks, 128), BF16),
+            V((2, slabs, toks, 128), BF16),
+            V((2, slabs, toks, 128), BF16),
+            V((2, slabs, toks, 128), BF16),
+            V((2, 2, slabs, toks, 128), BF16),
             dma((7,)),
-            dma((2, n)), dma((2, n)), dma((2,)), dma((2,)),
-            dma((2, n + 1)), dma((2, n + 1)),
-            dma((2, chunks)), dma((2, chunks)),
-            dma((2, chunks, n)), dma((2, chunks, n)),
-            dma((2, chunks)), dma((2, chunks)), dma((2, chunks)), dma((2, chunks)),
-            dma((2, chunks)), dma((2, chunks)), dma((2, chunks)), dma((2, chunks)),
+            dma((2, 2)), dma((2, 2, n - 1)), dma((2,)), dma((2, 2)),
+            dma((2,)), dma((2, 2)),
+            dma((2,)), dma((2, half // wide)),
+            dma((2,)), dma((2, most)),
+            dma((2,)), dma((2, most)), dma((2,)), dma((2, most)), dma((2,)), dma((2, most)),
         ],
         compiler_params=pltpu.CompilerParams(
             collective_id=0, has_side_effects=True, vmem_limit_bytes=54 * 1000 * 1000

time: 68.9 us -> 62.5 us (0.907)
  Pallas kernels: 67.9 us -> 61.6 us
    pallas_call x1, Pallas kernels: 60.3 us -> 54 us  [fused(): pl.pallas_call(functools.partial(routed_kernel, n, cap, tile, wide, piece...]
where the time goes in v2:
time: 62.5 us; the launch traced here: 62.4 us
  Pallas kernels  61.6 us (99%)
  between operations  0.8 us (1%)
    pallas_call x1, Pallas kernels, fused(): pl.pallas_call(functools.partial(routed_kernel, n, cap, tile, wide, piece...  54 us
    pallas_call x1, Pallas kernels, fused(): pl.pallas_call(functools.partial(grads_kernel, step), out_shape=(jax.Shap...  7.54 us

profile of v2, /device:TPU:0, one launch (start us, length us, event | category | flops | bytes accessed | tf_op | source)
XLA Modules:
  0.0 62.4 jit_solution(7087109561350459540)
XLA Ops:
  0.6 54.0 %routed.1 = (bf16[128,3072]{1,0:T(8,128)(2,1)S(1)}, bf16[128,3072]{1,0:T(8,128)(2,1)S(1)}, bf16[3072,256]{1,0:T(8,128)(2,1)S(1)}, bf16[256,3072]{1,0:T(8,128)(2,...) custom-call(bf16[128,3072]{1,0:T(8,128)(2,1)} %tokens_hbm.1, bf16[128,3072]{1,0:T(8,128)(2,1)} %cotangent_hbm.1, ...), custom_call_target="tpu_custom_call" | custom-call | tf_op jit(solution)/shard_map/routed/pallas_call | solution.py:550
  54.7 7.5 %grads.1 = (bf16[128,3072]{1,0:T(8,128)(2,1)}, bf16[128,3072]{1,0:T(8,128)(2,1)}, bf16[3072,1024]{1,0:T(8,128)(2,1)}, bf16[3072,1024]{1,0:T(8,128)(2,1)}, bf16[1024,3072]{1,0:T(8,128)(2,1)}) custom-call(bf16[128,3072]{1,0:T(8,128)(2,1)S(1)} %get-tuple-element.16.output, bf16[128,3072]{1,0:T(8,128)(2,1)S(1)} %get-tuple-element.17.input_grad, ...), custom_call_target="tpu_custom_call" | custom-call | tf_op jit(solution)/shard_map/grads/pallas_call | solution.py:600

commit v3 on v2

--- a/solution.py
+++ b/solution.py
@@ -38,13 +38,13 @@
 
 
 def routed_kernel(
-    n, cap, tile, wide, pieces,
+    n, cap, tile, spans, pieces, shares,
     tokens_hbm, cotangent_hbm, routes_hbm, rweight_hbm, wg_hbm, wu_hbm, wd_hbm,
     output, input_grad, x_turned, dy_rows, hid_turned, hid_dy,
     tok, cot, rts, rwt, wg, wu, wd, slots, snd, gpre, upre, hacc, hid,
     core_snd, core_rcv, own, ret_snd, ret, part, from_outer, joint, from_inner, fin,
     w_sem, a_send, a_recv, d_send, d_recv, f_send, f_recv, c_send, c_recv, r_send, r_recv,
-    s_send, s_recv, j_send, j_recv, h_send, h_recv,
+    s_send, s_recv, j_send, j_recv, h_send, h_recv, x_send, x_recv,
 ):
     d = lax.axis_index("dp")
     f = lax.axis_index("fsdp")
@@ -53,6 +53,7 @@
     sib = (d, flip(f, 1))
     pair = (d, flip(f, 2))
     across = (d, 2 * (3 - z) + c)
+    skew = (d, flip(f, 3))
     outer = (z % 3) == 0
     inner = (z % 3) != 0
     toks, features = tok.shape
@@ -72,7 +73,7 @@
         )
 
     barrier = pltpu.get_barrier_semaphore()
-    friends = [(flip(d, m), f) for m in order] + [sib, pair, across]
+    friends = [(flip(d, m), f) for m in order] + [sib, pair, across, skew]
     for dev in friends:
         pl.semaphore_signal(barrier, inc=1, device_id=dev, device_id_type=MESH)
 
@@ -132,7 +133,7 @@
 
     held = pl.ds(pl.multiple_of((z % 2) * share, 16), share)
     missing = pl.ds(pl.multiple_of((1 - z % 2) * share, 16), share)
-    parts = 2
+    parts = a_recv.shape[1]
     depth = half // parts
 
     def part_of(j):
@@ -205,86 +206,59 @@
         upre[at, cols] = u
         hid[at, cols] = (g * jax.nn.sigmoid(g) * u).astype(BF16)
 
-    self_rows = pl.ds(0, cap)
-    their_rows = pl.ds(cap, rows - cap)
-
-    def self_gate(j, carry):
-        cols = pl.ds(j * tile, tile)
-        gpre[self_rows, cols] = mm(slots[0, 0, 0], wg[pl.ds(0, half), cols]) + mm(
-            slots[1, 0, 0], wg[pl.ds(half, half), cols]
+    def gate_up(m0, blocks, h, k, first=False, final=False):
+        at = pl.ds(m0 * cap, blocks * cap)
+        depth_at = pl.ds(pl.multiple_of(h * half + k * depth, 128), depth)
+        for j in range(units // tile):
+            cols = pl.ds(j * tile, tile)
+            x = slots[h, 0, m0 : m0 + blocks, :, part_of(k)].reshape(blocks * cap, depth)
+            g = mm(x, wg[depth_at, cols])
+            u = mm(x, wu[depth_at, cols])
+            if not first:
+                g = g + gpre[at, cols]
+                u = u + upre[at, cols]
+            gpre[at, cols] = g
+            upre[at, cols] = u
+            if final:
+                hid[at, cols] = (g * jax.nn.sigmoid(g) * u).astype(BF16)
+
+    def scoped(what, *args, **kw):
+        with jax.named_scope(what.__name__ + "".join(str(a) for a in args if isinstance(a, int))):
+            what(*args, **kw)
+
+    loads[4].wait()
+    loads[5].wait()
+    for i in range(2 * parts):
+        scoped(
+            gate_up, 0, 1, c if i < parts else 1 - c, i % parts,
+            first=i == 0, final=i == 2 * parts - 1,
         )
-        return carry
-
-    def self_up(j, carry):
-        cols = pl.ds(j * tile, tile)
-        u = mm(slots[0, 0, 0], wu[pl.ds(0, half), cols]) + mm(
-            slots[1, 0, 0], wu[pl.ds(half, half), cols]
+    for j in range(parts):
+        scoped(relay_far, 0, j)
+    others = n - 1
+    for j in range(parts):
+        scoped(collect, 0, j)
+        scoped(gate_up, 1, others, c, j, first=j == 0)
+        if 0 < j < parts - 1:
+            scoped(collected, 0, j - 1)
+            scoped(gate_up, 1, others, 1 - c, j - 1)
+    for j in range(max(0, parts - 2), parts):
+        scoped(collected, 0, j)
+        scoped(gate_up, 1, others, 1 - c, j, final=j == parts - 1)
+        if j < parts - 1:
+            for k in range(parts - 1):
+                scoped(relay_far, 1, k)
+    scoped(relay_far, 1, parts - 1)
+    loads[6].wait()
+
+    def span(t, k):
+        return pl.ds(spans[t][k][0] * 128, spans[t][k][1] * 128)
+
+    def swap(t, k):
+        at = span(t, k)
+        return remote(
+            core_snd.at[t, :, at], core_rcv.at[t, :, at], c_send.at[t], c_recv.at[t, k], sib
         )
-        activate(self_rows, cols, gpre[self_rows, cols], u)
-        return carry
-
-    def near_part(h, k, j, carry):
-        cols = pl.ds(j * tile, tile)
-        x = slots[h, 0, 1:, :, part_of(k)].reshape(rows - cap, depth)
-        at = pl.ds(pl.multiple_of(h * half + k * depth, 128), depth)
-        gpre[their_rows, cols] += mm(x, wg[at, cols])
-        upre[their_rows, cols] += mm(x, wu[at, cols])
-        return carry
-
-    def first_part(j, carry):
-        cols = pl.ds(j * tile, tile)
-        x = slots[c, 0, 1:, :, part_of(0)].reshape(rows - cap, depth)
-        at = pl.ds(pl.multiple_of(c * half, 128), depth)
-        gpre[their_rows, cols] = mm(x, wg[at, cols])
-        upre[their_rows, cols] = mm(x, wu[at, cols])
-        return carry
-
-    def last_part(j, carry):
-        cols = pl.ds(j * tile, tile)
-        x = slots[1 - c, 0, 1:, :, part_of(parts - 1)].reshape(rows - cap, depth)
-        at = pl.ds(pl.multiple_of((1 - c) * half + (parts - 1) * depth, 128), depth)
-        g = gpre[their_rows, cols] + mm(x, wg[at, cols])
-        u = upre[their_rows, cols] + mm(x, wu[at, cols])
-        activate(their_rows, cols, g, u)
-        return carry
-
-    def each_tile(body):
-        for j in range(units // tile):
-            body(j, 0)
-
-    loads[4].wait()
-    with jax.named_scope("self_gate"):
-        each_tile(self_gate)
-    loads[5].wait()
-    with jax.named_scope("self_up"):
-        each_tile(self_up)
-    with jax.named_scope("relay0"):
-        relay_far(0, 0)
-        relay_far(0, 1)
-    with jax.named_scope("collect00"):
-        collect(0, 0)
-    with jax.named_scope("own0"):
-        each_tile(first_part)
-    with jax.named_scope("collect01"):
-        collect(0, 1)
-    with jax.named_scope("own1"):
-        each_tile(functools.partial(near_part, c, 1))
-    with jax.named_scope("collected00"):
-        collected(0, 0)
-    with jax.named_scope("relay10"):
-        relay_far(1, 0)
-    with jax.named_scope("sib0"):
-        each_tile(functools.partial(near_part, 1 - c, 0))
-    with jax.named_scope("collected01"):
-        collected(0, 1)
-    with jax.named_scope("relay11"):
-        relay_far(1, 1)
-    with jax.named_scope("sib1"):
-        each_tile(last_part)
-    loads[6].wait()
-
-    def swap(t, k):
-        return remote(core_snd.at[t, k], core_rcv.at[t, k], c_send.at[t], c_recv.at[t, k], sib)
 
     def returned(t, q, m):
         at = pl.ds(*pieces[t][q])
@@ -292,73 +266,75 @@
             ret_snd.at[t, at, m], ret.at[t, at, m], r_send.at[t], r_recv.at[t, q], (flip(d, m), f)
         )
 
-    per = wide // 128
-
     def term(t, cols):
         if t == 0:
             return mm(hid[...], wd[:, cols])
         return mm(hid_dy[0], wg[cols, :], TRAIL) + mm(hid_dy[1], wu[cols, :], TRAIL)
 
     def theirs(t, k):
-        at = pl.multiple_of((1 - c) * half + k * wide, 128)
-        core_snd[t, k] = term(t, pl.ds(at, wide)).astype(BF16)
+        g0, size = spans[t][k]
+        at = pl.multiple_of((1 - c) * half + g0 * 128, 128)
+        core_snd[t, :, span(t, k)] = term(t, pl.ds(at, size * 128)).astype(BF16)
         swap(t, k).start()
 
     def ours(t, k):
-        at = pl.multiple_of(c * half + k * wide, 128)
-        own[t, k] = term(t, pl.ds(at, wide))
+        g0, size = spans[t][k]
+        at = pl.multiple_of(c * half + g0 * 128, 128)
+        own[t, :, span(t, k)] = term(t, pl.ds(at, size * 128))
 
     def finish(t, k):
         swap(t, k).wait_recv()
+        low, size = spans[t][k]
         for q, (g0, count) in enumerate(pieces[t]):
-            if g0 // per != k:
+            if not low <= g0 < low + size:
                 continue
             for m in order + [0]:
                 for g in range(g0, g0 + count):
-                    at = (g - k * per) * 128
-                    rows_at = pl.ds(m * cap, cap)
-                    v = own[t, k, rows_at, at : at + 128] + core_rcv[
-                        t, k, rows_at, at : at + 128
-                    ].astype(F32)
+                    cols = pl.ds(g * 128, 128)
+                    at = pl.ds(m * cap, cap)
+                    v = own[t, at, cols] + core_rcv[t, at, cols].astype(F32)
                     (ret_snd if m else ret)[t, g, m] = v.astype(BF16)
                 if m:
                     returned(t, q, m).start()
 
     def down_own():
-        def body(j, carry):
+        for j in range(units // tile):
             cols = pl.ds(j * tile, tile)
             hacc[:, cols] = mm(slots[c, 1].reshape(rows, half), wd[cols, mine], TRAIL)
-            return carry
-
-        each_tile(body)
-
-    def down_rest():
-        def body(j, carry):
-            cols = pl.ds(j * tile, tile)
-            hdy = hacc[:, cols] + mm(slots[1 - c, 1].reshape(rows, half), wd[cols, other], TRAIL)
-            g = gpre[:, cols]
-            sig = jax.nn.sigmoid(g)
-            hid_dy[0, :, cols] = (hdy * upre[:, cols] * sig * (1.0 + g * (1.0 - sig))).astype(BF16)
-            hid_dy[1, :, cols] = (hdy * (g * sig)).astype(BF16)
-            return carry
-
-        each_tile(body)
-
-    def outward(t, q):
-        at = pl.ds(*pieces[t][q])
-        return remote(part.at[t, at], from_outer.at[t, at], s_send.at[t], s_recv.at[t, q], pair)
-
-    def middle(t, q):
-        at = pl.ds(*pieces[t][q])
-        return remote(joint.at[t, at], from_inner.at[t, at], j_send.at[t], j_recv.at[t, q], across)
-
-    def spread(t, q):
-        piece = fin.at[c, t, pl.ds(*pieces[t][q])]
-        return remote(piece, piece, s_send.at[t], s_recv.at[t, q], pair)
-
-    def last(t, q, h):
-        piece = fin.at[h, t, pl.ds(*pieces[t][q])]
-        return remote(piece, piece, h_send.at[t], h_recv.at[t, q], sib)
+
+    def down_rest(j):
+        cols = pl.ds(j * tile, tile)
+        hdy = hacc[:, cols] + mm(slots[1 - c, 1].reshape(rows, half), wd[cols, other], TRAIL)
+        g = gpre[:, cols]
+        sig = jax.nn.sigmoid(g)
+        hid_dy[0, :, cols] = (hdy * upre[:, cols] * sig * (1.0 + g * (1.0 - sig))).astype(BF16)
+        hid_dy[1, :, cols] = (hdy * (g * sig)).astype(BF16)
+
+    def outward(t, g):
+        return remote(part.at[t, g], from_outer.at[t, g], s_send.at[t], s_recv.at[t, g], pair)
+
+    def middle(t, g):
+        return remote(joint.at[t, g], from_inner.at[t, g], j_send.at[t], j_recv.at[t, g], across)
+
+    def spread(t, g):
+        piece = fin.at[c, t, g]
+        return remote(piece, piece, s_send.at[t], s_recv.at[t, g], pair)
+
+    def last(t, k, h):
+        piece = fin.at[h, t, pl.ds(*shares[t][k])]
+        return remote(piece, piece, h_send.at[t], h_recv.at[t, k], sib)
+
+    def spread_skew(h):
+        piece = fin.at[h, 1, slabs - 1]
+        return remote(piece, piece, x_send.at[0], x_recv.at[0], skew)
+
+    final = (1, len(shares[1]) - 1)
+
+    def share_of(t, g):
+        for k, (g0, size) in enumerate(shares[t]):
+            if g == g0 + size - 1:
+                return k
+        return None
 
     def combine(t, q):
         g0, count = pieces[t][q]
@@ -373,37 +349,52 @@
 
         @pl.when(outer)
         def _():
-            outward(t, q).start()
-
-    def join(t, q):
-        at = pl.ds(*pieces[t][q])
-
+            for i in range(count):
+                outward(t, g0 + i).start()
+
+    def join(t, g):
         @pl.when(inner)
         def _():
-            outward(t, q).wait_recv()
-            joint[t, at] = (part[t, at].astype(F32) + from_outer[t, at].astype(F32)).astype(BF16)
-            middle(t, q).start()
-
-    def settle(t, q):
-        at = pl.ds(*pieces[t][q])
+            outward(t, g).wait_recv()
+            joint[t, g] = (part[t, g].astype(F32) + from_outer[t, g].astype(F32)).astype(BF16)
+            middle(t, g).start()
+
+    def settle(t, g):
+        k = share_of(t, g)
 
         @pl.when(inner)
         def _():
-            middle(t, q).wait_recv()
-            v = joint[t, at].astype(F32) + from_inner[t, at].astype(F32)
-            fin[c, t, at] = v.astype(BF16)
-            spread(t, q).start()
-            last(t, q, c).start()
-
-    def arrive(t, q):
+            middle(t, g).wait_recv()
+            v = joint[t, g].astype(F32) + from_inner[t, g].astype(F32)
+            fin[c, t, g] = v.astype(BF16)
+            spread(t, g).start()
+            if (t, k) == final:
+                spread_skew(c).start()
+            if k is not None:
+                last(t, k, c).start()
+
+    def arrive(t, g):
+        k = share_of(t, g)
+
         @pl.when(outer)
         def _():
-            spread(t, q).wait_recv()
-            last(t, q, c).start()
-
-    def place(t, q):
-        last(t, q, 1 - c).wait_recv()
-        g0, count = pieces[t][q]
+            spread(t, g).wait_recv()
+            if k is not None and (t, k) != final:
+                last(t, k, c).start()
+
+    def place(t, k):
+        if (t, k) == final:
+
+            @pl.when(outer)
+            def _():
+                spread_skew(1 - c).wait_recv()
+
+            @pl.when(inner)
+            def _():
+                last(t, k, 1 - c).wait_recv()
+        else:
+            last(t, k, 1 - c).wait_recv()
+        g0, count = shares[t][k]
         for h in range(2):
             for g in range(g0, g0 + count):
                 at = h * half + g * 128
@@ -427,40 +418,44 @@
         for j in range(parts):
             collected(1, j)
 
-    count = half // wide
     plan = []
 
     def at(when, what, *args):
         plan.append((when, len(plan), what, args))
 
-    def project(t, when, unit, end):
-        for k in range(count):
-            at(when + 2 * k * unit, theirs, t, k)
-            if k:
-                at(when + 2 * k * unit + 0.01, finish, t, k - 1)
-            at(when + (2 * k + 1) * unit, ours, t, k)
-        at(end, finish, t, count - 1)
+    def project(t, send_at, keep_at, done_at):
+        for k in range(len(spans[t])):
+            at(send_at[k], theirs, t, k)
+            at(keep_at[k], ours, t, k)
+            at(done_at[k], finish, t, k)
 
     beat = 0.7
-    lag = 2.3
-    project(0, 0.0, 0.46, 4.2)
-    at(2.9, gather)
-    at(3.0, down_own)
-    at(4.25, gathered)
-    at(4.3, down_rest)
-    project(1, 5.6, 0.76, 11.2)
+    lag = 2.8
+    project(0, (0.0, 0.9, 1.9), (0.45, 1.45, 2.4), (1.4, 2.35, 4.5))
+    at(2.85, gather)
+    at(3.6, down_own)
+    at(4.55, gathered)
+    for j in range(units // tile):
+        at(4.6 + 0.9 * j, down_rest, j)
+    project(1, (6.4, 8.3, 10.35), (7.6, 9.0, 11.1), (8.31, 10.34, 12.4))
     for k in range(6):
-        at(12.0 + k, turn, k)
+        at(12.8 + k, turn, k)
     free = [0.0] * 4
-    ready = [1.5, 8.2]
+    ready = [1.4, 9.2]
     for t in range(2):
         for q, (g0, size) in enumerate(pieces[t]):
-            when = ready[t]
-            for i, act in enumerate((combine, join, settle, arrive)):
-                free[i] = max(free[i], when) + beat * size
-                when = free[i] + lag + (1.0 if i == 0 else 0.0)
-                at(when + (1.5 if act is arrive else 0.0), act, t, q)
-            at(when + 2.8, place, t, q)
+            free[0] = max(free[0], ready[t]) + beat * size
+            landed = free[0] + lag + 0.5
+            at(4.52 if t == 0 and q == 0 else landed, combine, t, q)
+            for g in range(g0, g0 + size):
+                when = landed
+                for i, act in enumerate((join, settle, arrive)):
+                    free[i + 1] = max(free[i + 1], when) + beat
+                    when = free[i + 1] + lag
+                    at(when + (1.5 if act is arrive else 0.0), act, t, g)
+                k = share_of(t, g)
+                if k is not None:
+                    at(when + 2.8, place, t, k)
     for _, _, what, args in sorted(plan, key=lambda e: e[:2]):
         with jax.named_scope(what.__name__ + "".join(str(a) for a in args)):
             what(*args)
@@ -478,16 +473,20 @@
             remote(core_snd.at[t], core_rcv.at[t], c_send.at[t], c_recv.at[t, 0], sib).wait_send()
             sent = ret_snd.at[t, :, pl.ds(1, n - 1)]
             remote(sent, sent, r_send.at[t], r_recv.at[t, 0], sib).wait_send()
-            sent = fin.at[c, t]
-            remote(sent, sent, h_send.at[t], h_recv.at[t, 0], sib).wait_send()
+            full = fin.at[c, t]
+            short = fin.at[c, t, pl.ds(0, slabs - 1)] if t else full
 
             @pl.when(outer)
             def _():
+                remote(short, short, h_send.at[t], h_recv.at[t, 0], sib).wait_send()
                 sent = part.at[t]
                 remote(sent, sent, s_send.at[t], s_recv.at[t, 0], pair).wait_send()
 
             @pl.when(inner)
             def _():
+                remote(full, full, h_send.at[t], h_recv.at[t, 0], sib).wait_send()
+                if t:
+                    spread_skew(c).wait_send()
                 sent = joint.at[t]
                 remote(sent, sent, j_send.at[t], j_recv.at[t, 0], across).wait_send()
                 sent = fin.at[c, t]
@@ -538,17 +537,26 @@
     half = features // 2
     units = w_gate.shape[2]
     tile = 512
-    wide = 512
+    parts = 2
     slabs = half // 128
+    third = slabs // 3
     even = [(g, 2) for g in range(0, slabs, 2)]
     pieces = ([(0, 1), (1, 1)] + even[1:], even[:-1] + [(slabs - 2, 1), (slabs - 1, 1)])
     most = max(len(p) for p in pieces)
+    spans = (
+        [(k * third, third) for k in range(3)],
+        [(k * third, third) for k in range(3)],
+    )
+    shares = (
+        [(k * third, third) for k in range(3)],
+        [(0, third), (third, third), (2 * third, third - 2), (slabs - 2, 1), (slabs - 1, 1)],
+    )
     vmem = pl.BlockSpec(memory_space=pltpu.VMEM)
     hbm = pl.BlockSpec(memory_space=pl.ANY)
     dma = pltpu.SemaphoreType.DMA
     V = pltpu.VMEM
     held = pl.pallas_call(
-        functools.partial(routed_kernel, n, cap, tile, wide, pieces),
+        functools.partial(routed_kernel, n, cap, tile, spans, pieces, shares),
         out_shape=(
             V((toks, features), BF16),
             V((toks, features), BF16),
@@ -573,9 +581,9 @@
             V((rows, units), F32),
             V((rows, units), F32),
             V((rows, units), BF16),
-            V((2, half // wide, rows, wide), BF16),
-            V((2, half // wide, rows, wide), BF16),
-            V((2, half // wide, rows, wide), F32),
+            V((2, rows, half), BF16),
+            V((2, rows, half), BF16),
+            V((2, rows, half), F32),
             V((2, slabs, n, cap, 128), BF16),
             V((2, slabs, n, cap, 128), BF16),
             V((2, slabs, toks, 128), BF16),
@@ -584,11 +592,12 @@
             V((2, slabs, toks, 128), BF16),
             V((2, 2, slabs, toks, 128), BF16),
             dma((7,)),
-            dma((2, 2)), dma((2, 2, n - 1)), dma((2,)), dma((2, 2)),
-            dma((2,)), dma((2, 2)),
-            dma((2,)), dma((2, half // wide)),
+            dma((2, 2)), dma((2, parts, n - 1)), dma((2,)), dma((2, parts)),
+            dma((2,)), dma((2, parts)),
+            dma((2,)), dma((2, 3)),
             dma((2,)), dma((2, most)),
-            dma((2,)), dma((2, most)), dma((2,)), dma((2, most)), dma((2,)), dma((2, most)),
+            dma((2,)), dma((2, slabs)), dma((2,)), dma((2, slabs)), dma((2,)), dma((2, 5)),
+            dma((1,)), dma((1,)),
         ],
         compiler_params=pltpu.CompilerParams(
             collective_id=0, has_side_effects=True, vmem_limit_bytes=54 * 1000 * 1000

time: 62.5 us -> 59.7 us (0.955)
  Pallas kernels: 61.6 us -> 58.8 us
    pallas_call x1, Pallas kernels: 54 us -> 51.2 us  [fused(): pl.pallas_call(functools.partial(routed_kernel, n, cap, tile, spans, piec...]
where the time goes in v3:
time: 59.7 us; the launch traced here: 59.6 us
  Pallas kernels  58.8 us (98%)
  between operations  0.8 us (1%)
    pallas_call x1, Pallas kernels, fused(): pl.pallas_call(functools.partial(routed_kernel, n, cap, tile, spans, piec...  51.2 us
    pallas_call x1, Pallas kernels, fused(): pl.pallas_call(functools.partial(grads_kernel, step), out_shape=(jax.Shap...  7.54 us

profile of v3, /device:TPU:0, one launch (start us, length us, event | category | flops | bytes accessed | tf_op | source)
XLA Modules:
  0.0 59.6 jit_solution(14715533731126095122)
XLA Ops:
  0.6 51.2 %routed.1 = (bf16[128,3072]{1,0:T(8,128)(2,1)S(1)}, bf16[128,3072]{1,0:T(8,128)(2,1)S(1)}, bf16[3072,256]{1,0:T(8,128)(2,1)S(1)}, bf16[256,3072]{1,0:T(8,128)(2,...) custom-call(bf16[128,3072]{1,0:T(8,128)(2,1)} %tokens_hbm.1, bf16[128,3072]{1,0:T(8,128)(2,1)} %cotangent_hbm.1, ...), custom_call_target="tpu_custom_call" | custom-call | tf_op jit(solution)/shard_map/routed/pallas_call | solution.py:558
  51.9 7.5 %grads.1 = (bf16[128,3072]{1,0:T(8,128)(2,1)}, bf16[128,3072]{1,0:T(8,128)(2,1)}, bf16[3072,1024]{1,0:T(8,128)(2,1)}, bf16[3072,1024]{1,0:T(8,128)(2,1)}, bf16[1024,3072]{1,0:T(8,128)(2,1)}) custom-call(bf16[128,3072]{1,0:T(8,128)(2,1)S(1)} %get-tuple-element.16.output, bf16[128,3072]{1,0:T(8,128)(2,1)S(1)} %get-tuple-element.17.input_grad, ...), custom_call_target="tpu_custom_call" | custom-call | tf_op jit(solution)/shard_map/grads/pallas_call | solution.py:609

commit v4 on v3

--- a/solution.py
+++ b/solution.py
@@ -322,7 +322,7 @@
 
     def last(t, k, h):
         piece = fin.at[h, t, pl.ds(*shares[t][k])]
-        return remote(piece, piece, h_send.at[t], h_recv.at[t, k], sib)
+        return remote(piece, piece, h_send.at[t], h_recv.at[t + k], sib)
 
     def spread_skew(h):
         piece = fin.at[h, 1, slabs - 1]
@@ -478,13 +478,13 @@
 
             @pl.when(outer)
             def _():
-                remote(short, short, h_send.at[t], h_recv.at[t, 0], sib).wait_send()
+                remote(short, short, h_send.at[t], h_recv.at[t], sib).wait_send()
                 sent = part.at[t]
                 remote(sent, sent, s_send.at[t], s_recv.at[t, 0], pair).wait_send()
 
             @pl.when(inner)
             def _():
-                remote(full, full, h_send.at[t], h_recv.at[t, 0], sib).wait_send()
+                remote(full, full, h_send.at[t], h_recv.at[t], sib).wait_send()
                 if t:
                     spread_skew(c).wait_send()
                 sent = joint.at[t]
@@ -548,8 +548,8 @@
         [(k * third, third) for k in range(3)],
     )
     shares = (
-        [(k * third, third) for k in range(3)],
-        [(0, third), (third, third), (2 * third, third - 2), (slabs - 2, 1), (slabs - 1, 1)],
+        [(0, slabs)],
+        [(0, slabs - 4), (slabs - 4, 2), (slabs - 2, 1), (slabs - 1, 1)],
     )
     vmem = pl.BlockSpec(memory_space=pltpu.VMEM)
     hbm = pl.BlockSpec(memory_space=pl.ANY)
@@ -596,7 +596,7 @@
             dma((2,)), dma((2, parts)),
             dma((2,)), dma((2, 3)),
             dma((2,)), dma((2, most)),
-            dma((2,)), dma((2, slabs)), dma((2,)), dma((2, slabs)), dma((2,)), dma((2, 5)),
+            dma((2,)), dma((2, slabs)), dma((2,)), dma((2, slabs)), dma((2,)), dma((5,)),
             dma((1,)), dma((1,)),
         ],
         compiler_params=pltpu.CompilerParams(

time: 59.7 us -> 59.7 us (level)
  no operation moved by 1% of the time
where the time goes in v4:
time: 59.7 us; the launch traced here: 59.5 us
  Pallas kernels  58.7 us (98%)
  between operations  0.8 us (1%)
    pallas_call x1, Pallas kernels, fused(): pl.pallas_call(functools.partial(routed_kernel, n, cap, tile, spans, piec...  51.2 us
    pallas_call x1, Pallas kernels, fused(): pl.pallas_call(functools.partial(grads_kernel, step), out_shape=(jax.Shap...  7.54 us

profile of v4, /device:TPU:0, one launch (start us, length us, event | category | flops | bytes accessed | tf_op | source)
XLA Modules:
  0.0 59.5 jit_solution(9548794307009892812)
XLA Ops:
  0.6 51.2 %routed.1 = (bf16[128,3072]{1,0:T(8,128)(2,1)S(1)}, bf16[128,3072]{1,0:T(8,128)(2,1)S(1)}, bf16[3072,256]{1,0:T(8,128)(2,1)S(1)}, bf16[256,3072]{1,0:T(8,128)(2,...) custom-call(bf16[128,3072]{1,0:T(8,128)(2,1)} %tokens_hbm.1, bf16[128,3072]{1,0:T(8,128)(2,1)} %cotangent_hbm.1, ...), custom_call_target="tpu_custom_call" | custom-call | tf_op jit(solution)/shard_map/routed/pallas_call | solution.py:558
  51.8 7.5 %grads.1 = (bf16[128,3072]{1,0:T(8,128)(2,1)}, bf16[128,3072]{1,0:T(8,128)(2,1)}, bf16[3072,1024]{1,0:T(8,128)(2,1)}, bf16[3072,1024]{1,0:T(8,128)(2,1)}, bf16[1024,3072]{1,0:T(8,128)(2,1)}) custom-call(bf16[128,3072]{1,0:T(8,128)(2,1)S(1)} %get-tuple-element.16.output, bf16[128,3072]{1,0:T(8,128)(2,1)S(1)} %get-tuple-element.17.input_grad, ...), custom_call_target="tpu_custom_call" | custom-call | tf_op jit(solution)/shard_map/grads/pallas_call | solution.py:609
